TPU v7x, 128 devices: a whole 4x4x4 slice. The times are simulated.
128 devices in a mesh: tok: 16 (over z, x), mp: 8 (over y, core).
Axes of the slice: x: 4, y: 4, z: 4, core: 2. Of those that a mesh axis runs over, the one named last changes fastest.
Arguments:
- tokens: bfloat16 [6144, 2048], P('tok', 'mp'), may hold values from -120 to 120
- norm_gain: float32 [2048], replicated, may hold values from 0.5 to 1.5
- running_sq: float32 [2048], P('mp'), may hold values from 0.5 to 4
- gate_weight: bfloat16 [2048, 8192], P(None, 'mp'), may hold values from -0.125 to 0.125
- up_weight: bfloat16 [2048, 8192], P(None, 'mp'), may hold values from -0.125 to 0.125
- down_weight_t: bfloat16 [2048, 8192], P(None, 'mp'), may hold values from -0.0625 to 0.0625
- groups: int32 [384], P('tok'), may hold values from 0 to 47, as said below
- cotangent: bfloat16 [6144, 2048], P('tok', 'mp'), may hold values from -6 to 6
Outputs:
- block_out: bfloat16 [6144, 2048], P('tok', 'mp')
- grad_tokens: bfloat16 [6144, 2048], P('tok', 'mp')
- running_new: float32 [2048], P('mp')
- grad_gain: float32 [2048], P('mp')
- grad_gate: float32 [2048, 8192], P('tok', 'mp')
- grad_up: float32 [2048, 8192], P('tok', 'mp')
- grad_down_t: float32 [2048, 8192], P('tok', 'mp')
Inputs may be any that keep to these rules, and one draw needn't show every extreme that they name: Each of the 48 ghost groups holds exactly 8 blocks.
All inputs are finite; a program needn't handle non-finite values.
Results may differ from a plain program's by a relative error of at most 0.02.
Values may be sent and summed in bfloat16 or wider, within the bound.
No kernel may reach another device: no remote copies, remote signals or barrier semaphores. Data moves between devices by JAX's collectives and lax.ppermute only.
A program may use at most 128 MiB of HBM per device.

v0:
```python
import jax
import jax.numpy as jnp
from jax import lax
from jax.experimental import pallas as pl
from jax.experimental.pallas import tpu as pltpu
from jax.sharding import Mesh
from jax.sharding import PartitionSpec as P


GHOST = 128
BLK = 16
RING = 4
NEAR = [(i, i ^ 1) for i in range(RING)]
FAR = [(i, RING - 1 - i) for i in range(RING)]
CORES = [(0, 1), (1, 0)]
EPSILON = 1e-05
MOMENTUM = 0.1


bf16 = jnp.bfloat16
f32 = jnp.float32


PATTERNS = (("z", 0), ("z", 1), ("x", 0), ("x", 1))
LENT = 128


def halving(i, first):
    near, far = i ^ 1, RING - 1 - i
    p, q = (near, far) if first == 0 else (far, near)
    return [RING - 1 - p if first == 0 else p ^ 1, p, q, i]


def row_blocks(coords, pattern):
    major, first = pattern
    hz, hx = halving(coords[0], first), halving(coords[1], first)
    if major == "z":
        return [RING * a + b for a in hz for b in hx]
    return [RING * a + b for b in hx for a in hz]


def feature_blocks(coords, other):
    core = coords[3] if other == 0 else 1 - coords[3]
    return [2 * ((coords[2] + k) & (RING - 1)) + core for k in range(RING)]


def shift(k):
    return [(i, (i + k) % RING) for i in range(RING)]


def vmem_spec():
    return pl.BlockSpec(memory_space=pltpu.VMEM)


def smem_spec():
    return pl.BlockSpec(memory_space=pltpu.SMEM)


def in_hbm(x):
    return pltpu.with_memory_space_constraint(x, pltpu.HBM)


def gathered(x):
    near = [x]
    for k in (1, 3, 2):
        near.append(lax.ppermute(x, "y", shift(-k)))
    near = [near[0], near[1], near[3], near[2]]
    far = []
    for k in range(RING):
        far.append(lax.ppermute(near[k], "c", CORES))
    return near + far


def block_sum(value):
    return jnp.sum(value, axis=0, keepdims=True)


def own_gain(coords, gain, feat):
    return gain[:, pl.ds(pl.multiple_of((2 * coords[2] + coords[3]) * feat, feat), feat)]


def add_kernel(left, right, out):
    out[...] = left[...] + right[...]


def pair_added(left, right):
    return pl.pallas_call(
        add_kernel,
        out_shape=jax.ShapeDtypeStruct(left.shape, left.dtype),
        in_specs=[vmem_spec()] * 2,
        out_specs=vmem_spec(),
        compiler_params=limits(1),
        name="pair_added",
    )(left, right)


def tok_halves(x):
    for i, (axis, pairs) in enumerate((("z", NEAR), ("z", FAR), ("x", NEAR), ("x", FAR)), 1):
        came = lax.ppermute(x, axis, pairs)
        if i < 4:
            x = pair_added(x, came)
    return x, came


def ring_sum_kernel(*refs):
    ins, out = refs[:-1], refs[-1]
    out[...] = (ins[0][...] + ins[3][...]) + (ins[1][...] + ins[2][...])


def ring_pieces(x, axis):
    came = [x]
    for k in (1, 3, 2):
        came.append(lax.ppermute(x, axis, shift(k)))
    return came


def ring_sum(x, axis):
    pieces = ring_pieces(x, axis)
    return pl.pallas_call(
        ring_sum_kernel,
        out_shape=jax.ShapeDtypeStruct(x.shape, x.dtype),
        in_specs=[vmem_spec()] * RING,
        out_specs=vmem_spec(),
        compiler_params=limits(1),
        name="ring_sum",
    )(*pieces)


STAGE_CUTS = 4


def stage_kernel(*refs):
    count = (len(refs) - 1) // 2
    sems = refs[-1]
    copies = []
    for i in range(count):
        source, out = refs[i], refs[count + i]
        rows = source.shape[0] // STAGE_CUTS
        for j in range(STAGE_CUTS):
            part = pl.ds(j * rows, rows)
            copies.append(
                pltpu.make_async_copy(source.at[part], out.at[part], sems.at[i * STAGE_CUTS + j])
            )
    for copy in copies:
        copy.start()
    for copy in copies:
        copy.wait()


def staged(*weights):
    return pl.pallas_call(
        stage_kernel,
        out_shape=tuple(pltpu.VMEM(w.shape, w.dtype) for w in weights),
        in_specs=[pl.BlockSpec(memory_space=pltpu.HBM)] * len(weights),
        out_specs=(vmem_spec(),) * len(weights),
        scratch_shapes=[pltpu.SemaphoreType.DMA((STAGE_CUTS * len(weights),))],
        compiler_params=limits(1),
        name="staged",
    )(*[in_hbm(w) for w in weights])


def stats_kernel(groups, coords, tokens, cotangent, out, both):
    rows = tokens.shape[0]
    both[:rows, :] = tokens[...]
    both[rows:, :] = cotangent[...]
    out[...] = jnp.zeros_like(out)
    for b in range(rows // BLK):
        value = tokens[b * BLK : (b + 1) * BLK, :].astype(f32)
        row = pl.ds(groups[b], 1)
        out[row, :] = out[row, :] + block_sum(value * value)


def stats(groups, coords, tokens, cotangent, groups_total):
    rows, feat = tokens.shape
    return pl.pallas_call(
        stats_kernel,
        out_shape=(
            jax.ShapeDtypeStruct((groups_total, feat), f32),
            jax.ShapeDtypeStruct((2 * rows, feat), bf16),
        ),
        in_specs=[smem_spec(), smem_spec(), vmem_spec(), vmem_spec()],
        out_specs=(vmem_spec(),) * 2,
        compiler_params=limits(4),
        name="stats",
    )(in_hbm(groups), coords, in_hbm(tokens), in_hbm(cotangent))


def table_kernel(a, b, c, d, table, quad):
    quad_mean = ((a[...] + d[...]) + (b[...] + c[...])) * (1.0 / GHOST)
    quad[...] = quad_mean
    table[...] = lax.rsqrt(quad_mean + EPSILON)


def scale_table(pieces):
    out = jax.ShapeDtypeStruct(pieces[0].shape, f32)
    return pl.pallas_call(
        table_kernel,
        out_shape=(out, out),
        in_specs=[vmem_spec()] * RING,
        out_specs=(vmem_spec(),) * 2,
        compiler_params=limits(2),
        name="scale_table",
    )(*pieces)


def partial_kernel(groups, tokens, table, own, *refs):
    came, (grad, out) = refs[:-2], refs[-2:]
    feat = tokens.shape[1]
    total = own[:feat, :]
    for ref in came:
        total = total + ref[:feat, :].astype(f32)
    grad[...] = total.T
    out[...] = jnp.zeros_like(out)
    for b in range(tokens.shape[0] // BLK):
        rows = slice(b * BLK, (b + 1) * BLK)
        row = pl.ds(groups[b], 1)
        normed = tokens[rows, :].astype(f32) * table[row, :]
        out[row, :] = out[row, :] + block_sum(grad[rows, :] * normed)


def partials(groups, tokens, table, own, came):
    rows, feat = tokens.shape
    return pl.pallas_call(
        partial_kernel,
        out_shape=(
            jax.ShapeDtypeStruct((rows, feat), f32),
            jax.ShapeDtypeStruct(table.shape, f32),
        ),
        in_specs=[smem_spec()] + [vmem_spec()] * (3 + len(came)),
        out_specs=(vmem_spec(),) * 2,
        compiler_params=limits(6),
        name="partials",
    )(in_hbm(groups), tokens, table, own, *came)


def input_kernel(groups, coords, tokens, cotangent, gain, table, grad, mine, came, out, grad_gain, acc):
    partial = mine[...] + came[...]
    grad_gain[...] = jnp.sum(partial, axis=0, keepdims=True)
    gain_row = own_gain(coords, gain, tokens.shape[1])
    acc[...] = gain_row * partial * (1.0 / GHOST)
    for b in range(tokens.shape[0] // BLK):
        rows = slice(b * BLK, (b + 1) * BLK)
        row = pl.ds(groups[b], 1)
        scale = table[row, :]
        normed = tokens[rows, :].astype(f32) * scale
        inner = gain_row * grad[rows, :] - normed * acc[row, :]
        out[rows, :] = (cotangent[rows, :].astype(f32) + scale * inner).astype(bf16)


def input_grads(groups, coords, tokens, cotangent, gain, table, grad, mine, came):
    rows, feat = tokens.shape
    return pl.pallas_call(
        input_kernel,
        out_shape=(
            jax.ShapeDtypeStruct((rows, feat), bf16),
            jax.ShapeDtypeStruct((1, feat), f32),
        ),
        in_specs=[smem_spec(), smem_spec()] + [vmem_spec()] * 7,
        out_specs=(vmem_spec(),) * 2,
        scratch_shapes=[pltpu.VMEM(table.shape, f32)],
        compiler_params=limits(6),
        name="input_grads",
    )(in_hbm(groups), coords, tokens, cotangent, gain, table, grad, mine, came)


def branch_kernel(tokens, running, quad, own, *refs):
    came, (out, running_new) = refs[:-2], refs[-2:]
    feat = tokens.shape[1]
    total = own[feat:, :]
    for ref in came:
        total = total + ref[feat:, :].astype(f32)
    out[...] = (tokens[...].astype(f32) + total.T).astype(bf16)
    mean = jnp.sum(quad[...], axis=0, keepdims=True) / quad.shape[0]
    running_new[...] = (1.0 - MOMENTUM) * running[...] + MOMENTUM * mean


def branch_out(tokens, running, quad, own, came):
    return pl.pallas_call(
        branch_kernel,
        out_shape=(
            jax.ShapeDtypeStruct(tokens.shape, bf16),
            jax.ShapeDtypeStruct(running.shape, f32),
        ),
        in_specs=[vmem_spec()] * (4 + len(came)),
        out_specs=(vmem_spec(),) * 2,
        compiler_params=limits(6),
        name="branch_out",
    )(tokens, in_hbm(running), quad, own, *came)


def limits(mib):
    return pltpu.CompilerParams(vmem_limit_bytes=mib << 20)


def places(coords):
    return feature_blocks(coords, 0) + feature_blocks(coords, 1)


def cotangent_kernel(coords, *refs):
    pieces, (out, turned) = refs[:-2], refs[-2:]
    rows, width = out.shape[0], pieces[0].shape[1]
    for place, piece in zip(places(coords), pieces):
        first = pl.multiple_of(place * width, width)
        value = piece[rows:, :]
        out[:, pl.ds(first, width)] = value
        turned[pl.ds(first, width), :] = value.T


def normalize_kernel(groups, coords, gain, *refs):
    ins, (out, turned) = refs[:-2], refs[-2:]
    pieces, tables = ins[: len(ins) // 2], ins[len(ins) // 2 :]
    rows, width = out.shape[0], pieces[0].shape[1]
    for place, piece, table in zip(places(coords), pieces, tables):
        first = pl.multiple_of(place * width, width)
        gain_row = gain[:, pl.ds(first, width)]
        for b in range(rows // BLK):
            block = slice(b * BLK, (b + 1) * BLK)
            normed = piece[block, :].astype(f32) * table[pl.ds(groups[b], 1), :]
            out[block, pl.ds(first, width)] = (gain_row * normed).astype(bf16)
        turned[pl.ds(first, width), :] = out[:, pl.ds(first, width)].T


def assembled_shapes(pieces):
    rows, width = pieces[0].shape[0] // 2, pieces[0].shape[1] * len(pieces)
    return (jax.ShapeDtypeStruct((rows, width), bf16), jax.ShapeDtypeStruct((width, rows), bf16))


def cotangent_whole(coords, pieces):
    return pl.pallas_call(
        cotangent_kernel,
        out_shape=assembled_shapes(pieces),
        in_specs=[smem_spec()] + [vmem_spec()] * len(pieces),
        out_specs=(vmem_spec(), vmem_spec()),
        compiler_params=limits(12),
        name="cotangent_whole",
    )(coords, *pieces)


def normalized_whole(groups, coords, gain, pieces, tables):
    return pl.pallas_call(
        normalize_kernel,
        out_shape=assembled_shapes(pieces),
        in_specs=[smem_spec(), smem_spec()] + [vmem_spec()] * (1 + 2 * len(pieces)),
        out_specs=(vmem_spec(), vmem_spec()),
        compiler_params=limits(12),
        name="normalized_whole",
    )(in_hbm(groups), coords, gain, *pieces, *tables)


def rows_product(blocks, turned, right, outs, first):
    columns = slice(first, first + right.shape[1])
    half = len(blocks) // 2
    values = []
    for part in (blocks[:half], blocks[half:]):
        left = jnp.concatenate(
            [turned[pl.ds(pl.multiple_of(b * 128, 128), 128), :] for b in part], axis=0
        )
        values.append(jnp.dot(left, right, preferred_element_type=f32).astype(bf16))
    done = 0
    for out in outs:
        value, start = values[done // values[0].shape[0]], done % values[0].shape[0]
        out[:, columns] = value[start : start + out.shape[0], :]
        done += out.shape[0]


def hidden_kernel(p, lent):
    def kernel(coords, hid, hid_t, dy, dy_t, gate_w, up_w, down_w, hidden_t, ggi_t, gl_t, *outs):
        gate = jnp.dot(hid[...], gate_w[...], preferred_element_type=f32)
        lift = jnp.dot(hid[...], up_w[...], preferred_element_type=f32)
        grad = jnp.dot(dy[...], down_w[...], preferred_element_type=f32)
        sigma = jax.nn.sigmoid(gate)
        act = gate * sigma
        hidden = (act * lift).astype(bf16)
        ggi = (grad * lift * sigma * (1.0 + gate * (1.0 - sigma))).astype(bf16)
        gl = (grad * act).astype(bf16)
        own = row_blocks(coords, PATTERNS[p])
        rows_product(own, dy_t, hidden[:, lent:], outs[:3], 0)
        both = jnp.concatenate([ggi, gl], axis=1)
        rows_product(own, hid_t, both, outs[:3], hidden.shape[1] - lent)
        if lent:
            rows_product(row_blocks(coords, PATTERNS[0]), dy_t, hidden[:, :lent], outs[3:], 0)
        hidden_t[...] = hidden.T
        ggi_t[...] = ggi.T
        gl_t[...] = gl.T

    return kernel


def hidden_part(p, coords, hid, hid_t, dy, dy_t, gate_w, up_w, down_w):
    rows, width = hid.shape
    part = gate_w.shape[1] // RING
    lent = LENT if p == RING - 1 else 0

    def fixed(*shape):
        return pl.BlockSpec(shape, lambda i: (0, 0))

    weight = pl.BlockSpec((width, part), lambda i: (0, p))
    columns = 3 * part - lent
    shapes = [(part, rows)] * 3 + [(width // 4, columns)] * 2 + [(width // 2, columns)]
    shapes += [(width // 2, lent)] * 2 if lent else []
    return pl.pallas_call(
        hidden_kernel(p, lent),
        grid=(1,),
        out_shape=tuple(jax.ShapeDtypeStruct(shape, bf16) for shape in shapes),
        in_specs=[
            smem_spec(),
            fixed(rows, width),
            fixed(width, rows),
            fixed(rows, width),
            fixed(width, rows),
            weight,
            weight,
            weight,
        ],
        out_specs=tuple(fixed(*shape) for shape in shapes),
        compiler_params=limits(20),
        name="hidden_part",
    )(coords, hid, hid_t, dy, dy_t, gate_w, up_w, down_w)


def back_kernel(coords, *refs):
    acts, weights = refs[: 3 * RING], refs[3 * RING : 3 * RING + 3]
    outs, whole = refs[3 * RING + 3 : -1], refs[-1]
    feat, part = outs[0].shape[1], acts[0].shape[0]
    for j in range(3):
        for p in range(RING):
            whole[j, p * part : (p + 1) * part, :] = acts[j * RING + p][...]
    for other, out in ((1, outs[0]), (0, outs[1])):
        core = coords[3] if other == 0 else 1 - coords[3]

        def step(k, carry, core=core, out=out):
            block = 2 * ((coords[2] + k) & (RING - 1)) + core
            rows = pl.ds(pl.multiple_of(block * feat, feat), feat)
            terms = [
                jnp.dot(weight[rows, :], whole[j], preferred_element_type=f32)
                for j, weight in enumerate(weights)
            ]
            out[k] = (terms[0] + terms[1]).astype(bf16)
            out[RING + k] = terms[2].astype(bf16)
            return carry

        lax.fori_loop(0, RING, step, 0)


def back(coords, acts, weights):
    rows = acts[0][0].shape[1]
    feat = weights[0].shape[0] // (2 * RING)
    out = jax.ShapeDtypeStruct((2 * RING, feat, rows), bf16)
    return pl.pallas_call(
        back_kernel,
        in_specs=[smem_spec()] + [vmem_spec()] * (3 * RING + 3),
        out_specs=(vmem_spec(), vmem_spec()),
        out_shape=(out, out),
        scratch_shapes=[pltpu.VMEM((3, weights[0].shape[1], rows), bf16)],
        compiler_params=limits(20),
        name="back",
    )(coords, *[a for group in acts for a in group], *weights)


def chip_sum_kernel(near, other, own, *sends):
    feat = near.shape[1]
    for j in range(2):
        rows = slice(j * feat, (j + 1) * feat)
        own[rows, :] = near[j * RING].astype(f32) + other[j * RING].astype(f32)
        for k, send in enumerate(sends, 1):
            i = j * RING + k
            send[rows, :] = (near[i].astype(f32) + other[i].astype(f32)).astype(bf16)


def mp_scattered(far, near):
    other = lax.ppermute(far, "c", CORES)
    piece = (2 * near.shape[1], near.shape[2])
    own, *sends = pl.pallas_call(
        chip_sum_kernel,
        out_shape=(jax.ShapeDtypeStruct(piece, f32),)
        + (jax.ShapeDtypeStruct(piece, bf16),) * (RING - 1),
        in_specs=[vmem_spec()] * 2,
        out_specs=(vmem_spec(),) * RING,
        compiler_params=limits(8),
        name="chip_sum",
    )(near, other)
    came = []
    for k in (1, 3, 2):
        came.append(lax.ppermute(sends[k - 1], "y", shift(k)))
    return own, came


def split_kernel(*refs):
    ins, (send, kept) = refs[:-2], refs[-2:]
    half = send.shape[0]
    first = 0
    for keep, came in zip(ins[::2], ins[1::2]):
        columns = slice(first, first + keep.shape[1])
        send[:, columns] = (keep[:half, :].astype(f32) + came[:half, :].astype(f32)).astype(bf16)
        kept[:, columns] = (keep[half:, :].astype(f32) + came[half:, :].astype(f32)).astype(bf16)
        first += keep.shape[1]


def split_add(*pairs):
    rows = pairs[0].shape[0] // 2
    half = jax.ShapeDtypeStruct((rows, sum(a.shape[1] for a in pairs[::2])), bf16)
    return pl.pallas_call(
        split_kernel,
        out_shape=(half, half),
        in_specs=[vmem_spec()] * len(pairs),
        out_specs=(vmem_spec(),) * 2,
        compiler_params=limits(8),
        name="split_add",
    )(*pairs)


def half_kernel(half, count):
    def kernel(*refs):
        ins, outs = refs[:-count], refs[-count:]
        rows = ins[0].shape[0] // 2
        first = 0
        for keep, came in zip(ins[::2], ins[1::2]):
            mine = keep[half * rows : (half + 1) * rows, :]
            start = half * rows if came.shape[0] > rows else 0
            theirs = came[start : start + rows, :]
            columns = slice(first, first + keep.shape[1])
            total = (mine.astype(f32) + theirs.astype(f32)).astype(bf16)
            for i, out in enumerate(outs):
                out[:, columns] = total[i * out.shape[0] : (i + 1) * out.shape[0], :]
            first += keep.shape[1]

    return kernel


def half_add(half, count, *pairs):
    rows = pairs[0].shape[0] // 2 // count
    out = jax.ShapeDtypeStruct((rows, sum(a.shape[1] for a in pairs[::2])), bf16)
    return pl.pallas_call(
        half_kernel(half, count),
        out_shape=(out,) * count,
        in_specs=[vmem_spec()] * len(pairs),
        out_specs=(vmem_spec(),) * count,
        compiler_params=limits(6),
        name="half_add",
    )(*pairs)


def sections(part):
    runs = []
    for p in range(RING):
        lent = LENT if p == RING - 1 else 0
        runs.append([(0, p * part + lent, part - lent), (1, p * part, part), (2, p * part, part)])
    runs[0].append((0, (RING - 1) * part, LENT))
    return runs


def finish_kernel(*refs):
    ins, outs = refs[: 2 * RING], refs[2 * RING :]
    for p, runs in enumerate(sections(outs[0].shape[1] // RING)):
        total = ins[2 * p][...].astype(f32) + ins[2 * p + 1][...].astype(f32)
        first = 0
        for out, column, width in runs:
            outs[out][:, column : column + width] = total[:, first : first + width]
            first += width


def finished(pairs, width):
    rows = pairs[0][0].shape[0]
    out = jax.ShapeDtypeStruct((rows, width), f32)
    return pl.pallas_call(
        finish_kernel,
        out_shape=(out,) * 3,
        in_specs=[vmem_spec()] * (2 * RING),
        out_specs=(vmem_spec(),) * 3,
        compiler_params=limits(6),
        name="finished",
    )(*[a for pair in pairs for a in pair])


def body(tokens, norm_gain, running_sq, gate_weight, up_weight, down_weight_t, groups, cotangent):
    tok_rows, feat = tokens.shape
    groups_total = tok_rows * RING * RING // GHOST
    coords = jnp.stack([lax.axis_index(a) for a in ("z", "x", "y", "c")]).astype(jnp.int32)
    gain = norm_gain.reshape(1, -1)
    local, both = stats(groups, coords, tokens, cotangent, groups_total)
    pieces = gathered(both)
    sums = ring_pieces(ring_sum(local, "z"), "x")
    table, quad = scale_table(sums)
    tables = gathered(table)
    (down_weight_t,) = staged(down_weight_t)
    gate_weight, up_weight = staged(gate_weight, up_weight)
    dy_full, dy_turned = cotangent_whole(coords, pieces)
    hid_full, hid_turned = normalized_whole(groups, coords, gain, pieces, tables)
    parts = []
    for p in range(RING):
        parts.append(
            hidden_part(
                p, coords, hid_full, hid_turned, dy_full, dy_turned, gate_weight, up_weight, down_weight_t
            )
        )
    last = []
    for p, (major, first) in enumerate(PATTERNS):
        minor = "x" if major == "z" else "z"
        pair = (NEAR, FAR) if first == 0 else (FAR, NEAR)
        send_a, send_b, keep = parts[p][3:6]
        more = ()
        if p == 0:
            more = (parts[-1][7], lax.ppermute(parts[-1][6], major, pair[0]))
        came_a = lax.ppermute(send_a, major, pair[0])
        came_b = lax.ppermute(send_b, major, pair[0])
        send_a, send_b = half_add(0, 2, keep, came_a, *more)
        next_a = lax.ppermute(send_a, major, pair[1])
        next_b = lax.ppermute(send_b, major, pair[1])
        (keep,) = half_add(1, 1, keep, came_b, *more)
        (send,) = half_add(0, 1, keep, next_a)
        came = lax.ppermute(send, minor, pair[0])
        (keep,) = half_add(1, 1, keep, next_b)
        send, keep = split_add(keep, came)
        came = lax.ppermute(send, minor, pair[1])
        last.append((keep, came))
    grad_down_t, grad_gate, grad_up = finished(last, gate_weight.shape[1])

    far, near = back(
        coords,
        [[q[1] for q in parts], [q[2] for q in parts], [q[0] for q in parts]],
        [gate_weight, up_weight, down_weight_t],
    )
    kept, came_y = mp_scattered(far, near)
    grad, local = partials(groups, tokens, table, kept, came_y)
    mine, came = tok_halves(local)
    grad_tokens, grad_gain = input_grads(groups, coords, tokens, cotangent, gain, table, grad, mine, came)

    block_out, running_new = branch_out(tokens, running_sq.reshape(1, feat), quad, kept, came_y)
    return (
        block_out,
        grad_tokens,
        running_new.reshape(feat),
        grad_gain.reshape(feat),
        grad_gate,
        grad_up,
        grad_down_t,
    )


def solution(mesh):
    torus = Mesh(mesh.devices.reshape(RING, RING, RING, 2), ("z", "x", "y", "c"))
    tok, mp = ("z", "x"), ("y", "c")
    placed = (P(tok, mp), P(), P(mp), P(None, mp), P(None, mp), P(None, mp), P(tok), P(tok, mp))
    out = (P(tok, mp), P(tok, mp), P(mp), P(mp), P(tok, mp), P(tok, mp), P(tok, mp))

    return jax.shard_map(body, mesh=torus, in_specs=placed, out_specs=out, check_vma=False)
```

profile of v0, /device:TPU:24, one launch (start us, length us, event | category | flops | bytes accessed | tf_op | source)
XLA Modules:
  0.0 206.5 jit_solution(14800345469011847401)
XLA Ops:
  11.9 10.5 %collective-permute-done.6.refs_1_ = bf16[768,256]{1,0:T(8,128)(2,1)S(1)} collective-permute-done((bf16[768,256]{1,0:T(8,128)(2,1)S(1)}, bf16[768,256]{1,0:T(8,128)(2,1)S(1)}, u32[]{:S(2)}, u32[]{:S(2)}) %collective-permute-start.6) | collective-permute-done | bytes 393248 | tf_op jit(solution)/shard_map/ppermute | solution.py:66
  23.0 3.9 %collective-permute-start.2 = (f32[48,256]{1,0:T(8,128)S(1)}, f32[48,256]{1,0:T(8,128)S(1)}, u32[]{:S(2)}, u32[]{:S(2)}) collective-permute-start(f32[48,256]{1,0:T(8,128)S(1)} %get-tuple-element.74.refs_0_), channel_id=1, source_target_pairs={{0,64},{32,96},{64,0},{96,32},{1,65},{33,97},{65,1},{97,33},{2,66}... | collective-permute-start | bytes 147464 | tf_op jit(solution)/shard_map/ppermute | solution.py:113
  30.5 3.8 %collective-permute-done.3.b = f32[48,256]{1,0:T(8,128)S(1)} collective-permute-done((f32[48,256]{1,0:T(8,128)S(1)}, f32[48,256]{1,0:T(8,128)S(1)}, u32[]{:S(2)}, u32[]{:S(2)}) %collective-permute-start.3) | collective-permute-done | bytes 49184 | tf_op jit(solution)/shard_map/ppermute | solution.py:113
  35.8 2.5 %collective-permute-done.4.c = f32[48,256]{1,0:T(8,128)S(1)} collective-permute-done((f32[48,256]{1,0:T(8,128)S(1)}, f32[48,256]{1,0:T(8,128)S(1)}, u32[]{:S(2)}, u32[]{:S(2)}) %collective-permute-start.4) | collective-permute-done | bytes 49184 | tf_op jit(solution)/shard_map/ppermute | solution.py:113
  40.2 3.8 %collective-permute-done.5.d = f32[48,256]{1,0:T(8,128)S(1)} collective-permute-done((f32[48,256]{1,0:T(8,128)S(1)}, f32[48,256]{1,0:T(8,128)S(1)}, u32[]{:S(2)}, u32[]{:S(2)}) %collective-permute-start.5) | collective-permute-done | bytes 49184 | tf_op jit(solution)/shard_map/ppermute | solution.py:113
  44.1 5.3 %collective-permute-done.13.refs_9_ = f32[48,256]{1,0:T(8,128)S(1)} collective-permute-done((f32[48,256]{1,0:T(8,128)S(1)}, f32[48,256]{1,0:T(8,128)S(1)}, u32[]{:S(2)}, u32[]{:S(2)}) %collective-permute-start.13) | collective-permute-done | bytes 49184 | tf_op jit(solution)/shard_map/ppermute | solution.py:66
  49.6 5.4 %collective-permute-done.14.refs_10_ = f32[48,256]{1,0:T(8,128)S(1)} collective-permute-done((f32[48,256]{1,0:T(8,128)S(1)}, f32[48,256]{1,0:T(8,128)S(1)}, u32[]{:S(2)}, u32[]{:S(2)}) %collective-permute-start.14) | collective-permute-done | bytes 49184 | tf_op jit(solution)/shard_map/ppermute | solution.py:66
  55.0 4.1 %collective-permute-done.15.refs_11_ = f32[48,256]{1,0:T(8,128)S(1)} collective-permute-done((f32[48,256]{1,0:T(8,128)S(1)}, f32[48,256]{1,0:T(8,128)S(1)}, u32[]{:S(2)}, u32[]{:S(2)}) %collective-permute-start.15) | collective-permute-done | bytes 49184 | tf_op jit(solution)/shard_map/ppermute | solution.py:66
  62.3 3.5 %staged.2 = (bf16[2048,1024]{1,0:T(8,128)(2,1)S(1)}, bf16[2048,1024]{1,0:T(8,128)(2,1)S(1)}) custom-call(bf16[2048,1024]{1,0:T(8,128)(2,1)} %refs_0_.2, bf16[2048,1024]{1,0:T(8,128)(2,1)} %refs_1_.1), custom_call_target="tpu_custom_call" | custom-call | tf_op jit(solution)/shard_map/staged/pallas_call | solution.py:151
  68.2 4.0 %hidden_part.7 = (bf16[256,384]{1,0:T(8,128)(2,1)S(1)}, bf16[256,384]{1,0:T(8,128)(2,1)S(1)}, bf16[256,384]{1,0:T(8,128)(2,1)S(1)}, bf16[512,640]{1,0:T(8,128)(2...) custom-call(s32[4]{0:T(128)S(1)} %pad_add_fusion.coords, ...), custom_call_target="tpu_custom_call" | custom-call | tf_op jit(solution)/shard_map/hidden_part/pallas_call | solution.py:401
  72.2 3.0 %collective-permute-start.48 = (bf16[512,640]{1,0:T(8,128)(2,1)S(1)}, bf16[512,640]{1,0:T(8,128)(2,1)S(1)}, u32[]{:S(2)}, u32[]{:S(2)}) collective-permute-start(bf16[512,640]{1,0:T(8,128)(2,1)S(1)} %get-tuple-element.133), channel_id=1, source_target_pairs={{0,24},{8,16},{16,8},{24,0},{1,25},{9,17},{17,9},{25,1},{2,26},{10... | collective-permute-start | bytes 1966088 | tf_op jit(solution)/shard_map/ppermute | solution.py:604
  75.2 3.7 %hidden_part.6 = (bf16[256,384]{1,0:T(8,128)(2,1)S(1)}, bf16[256,384]{1,0:T(8,128)(2,1)S(1)}, bf16[256,384]{1,0:T(8,128)(2,1)S(1)}, bf16[512,768]{1,0:T(8,128)(2...) custom-call(s32[4]{0:T(128)S(1)} %pad_add_fusion.coords, ...), custom_call_target="tpu_custom_call" | custom-call | tf_op jit(solution)/shard_map/hidden_part/pallas_call | solution.py:401
  83.1 3.7 %hidden_part.5 = (bf16[256,384]{1,0:T(8,128)(2,1)S(1)}, bf16[256,384]{1,0:T(8,128)(2,1)S(1)}, bf16[256,384]{1,0:T(8,128)(2,1)S(1)}, bf16[512,768]{1,0:T(8,128)(2...) custom-call(s32[4]{0:T(128)S(1)} %pad_add_fusion.coords, ...), custom_call_target="tpu_custom_call" | custom-call | tf_op jit(solution)/shard_map/hidden_part/pallas_call | solution.py:401
  86.8 3.7 %hidden_part.4 = (bf16[256,384]{1,0:T(8,128)(2,1)S(1)}, bf16[256,384]{1,0:T(8,128)(2,1)S(1)}, bf16[256,384]{1,0:T(8,128)(2,1)S(1)}, bf16[512,768]{1,0:T(8,128)(2...) custom-call(s32[4]{0:T(128)S(1)} %pad_add_fusion.coords, ...), custom_call_target="tpu_custom_call" | custom-call | tf_op jit(solution)/shard_map/hidden_part/pallas_call | solution.py:401
  90.6 8.7 %back.1 = (bf16[8,256,384]{2,1,0:T(8,128)(2,1)S(1)}, bf16[8,256,384]{2,1,0:T(8,128)(2,1)S(1)}) custom-call(s32[4]{0:T(128)S(1)} %pad_add_fusion.coords, bf16[256,384]{1,0:T(8,128)(2,1)S(1)} %get-tuple-element.84.refs_0_, bf16[256,384]{1,0:T(8,128)(2,1)S(1)} %get-tuple-element.85.refs_1_, bf16[256,384]{1,0:T(8,128)(2,1)S(1)} %get-tuple-element.86.refs_2_, ...), custom_call_target="tpu_custom_call" | custom-call | tf_op jit(solution)/shard_map/back/pallas_call | solution.py:449
  99.6 2.6 %collective-permute-start.36 = (bf16[512,768]{1,0:T(8,128)(2,1)S(1)}, bf16[512,768]{1,0:T(8,128)(2,1)S(1)}, u32[]{:S(2)}, u32[]{:S(2)}) collective-permute-start(bf16[512,768]{1,0:T(8,128)(2,1)S(1)} %get-tuple-element.119), channel_id=1, source_target_pairs={{0,96},{32,64},{64,32},{96,0},{1,97},{33,65},{65,33},{97,1},{2,98}... | collective-permute-start | bytes 2359304 | tf_op jit(solution)/shard_map/ppermute | solution.py:604
  108.5 6.6 %collective-permute-done.41.refs_1_ = bf16[512,768]{1,0:T(8,128)(2,1)S(1)} collective-permute-done((bf16[512,768]{1,0:T(8,128)(2,1)S(1)}, bf16[512,768]{1,0:T(8,128)(2,1)S(1)}, u32[]{:S(2)}, u32[]{:S(2)}) %collective-permute-start.41) | collective-permute-done | bytes 786464 | tf_op jit(solution)/shard_map/ppermute | solution.py:605
  116.8 4.5 %collective-permute-done.36.refs_1_ = bf16[512,768]{1,0:T(8,128)(2,1)S(1)} collective-permute-done((bf16[512,768]{1,0:T(8,128)(2,1)S(1)}, bf16[512,768]{1,0:T(8,128)(2,1)S(1)}, u32[]{:S(2)}, u32[]{:S(2)}) %collective-permute-start.36) | collective-permute-done | bytes 786464 | tf_op jit(solution)/shard_map/ppermute | solution.py:604
  121.5 3.3 %collective-permute-done.30.refs_1_ = bf16[512,768]{1,0:T(8,128)(2,1)S(1)} collective-permute-done((bf16[512,768]{1,0:T(8,128)(2,1)S(1)}, bf16[512,768]{1,0:T(8,128)(2,1)S(1)}, u32[]{:S(2)}, u32[]{:S(2)}) %collective-permute-start.30) | collective-permute-done | bytes 786464 | tf_op jit(solution)/shard_map/ppermute | solution.py:604
  124.8 2.8 %collective-permute-start.44 = (bf16[256,768]{1,0:T(8,128)(2,1)S(1)}, bf16[256,768]{1,0:T(8,128)(2,1)S(1)}, u32[]{:S(2)}, u32[]{:S(2)}) collective-permute-start(bf16[256,768]{1,0:T(8,128)(2,1)S(1)} %get-tuple-element.128), channel_id=1, source_target_pairs={{0,24},{8,16},{16,8},{24,0},{1,25},{9,17},{17,9},{25,1},{2,26},{10... | collective-permute-start | bytes 1179656 | tf_op jit(solution)/shard_map/ppermute | solution.py:607
  127.8 9.8 %collective-permute-done.35.refs_1_ = bf16[512,768]{1,0:T(8,128)(2,1)S(1)} collective-permute-done((bf16[512,768]{1,0:T(8,128)(2,1)S(1)}, bf16[512,768]{1,0:T(8,128)(2,1)S(1)}, u32[]{:S(2)}, u32[]{:S(2)}) %collective-permute-start.35) | collective-permute-done | bytes 786464 | tf_op jit(solution)/shard_map/ppermute | solution.py:605
  140.1 2.8 %collective-permute-start.43 = (bf16[256,768]{1,0:T(8,128)(2,1)S(1)}, bf16[256,768]{1,0:T(8,128)(2,1)S(1)}, u32[]{:S(2)}, u32[]{:S(2)}) collective-permute-start(bf16[256,768]{1,0:T(8,128)(2,1)S(1)} %get-tuple-element.127), channel_id=1, source_target_pairs={{0,24},{8,16},{16,8},{24,0},{1,25},{9,17},{17,9},{25,1},{2,26},{10... | collective-permute-start | bytes 1179656 | tf_op jit(solution)/shard_map/ppermute | solution.py:608
  147.1 4.6 %collective-permute-done.43.refs_1_ = bf16[256,768]{1,0:T(8,128)(2,1)S(1)} collective-permute-done((bf16[256,768]{1,0:T(8,128)(2,1)S(1)}, bf16[256,768]{1,0:T(8,128)(2,1)S(1)}, u32[]{:S(2)}, u32[]{:S(2)}) %collective-permute-start.43) | collective-permute-done | bytes 393248 | tf_op jit(solution)/shard_map/ppermute | solution.py:608
  154.8 2.8 %collective-permute-start.39 = (bf16[256,768]{1,0:T(8,128)(2,1)S(1)}, bf16[256,768]{1,0:T(8,128)(2,1)S(1)}, u32[]{:S(2)}, u32[]{:S(2)}) collective-permute-start(bf16[256,768]{1,0:T(8,128)(2,1)S(1)} %half_add.23), channel_id=1, source_target_pairs={{0,24},{8,16},{16,8},{24,0},{1,25},{9,17},{17,9},{25,1},{2,26},{10... | collective-permute-start | bytes 1179656 | tf_op jit(solution)/shard_map/ppermute | solution.py:611
  158.0 5.6 %collective-permute-done.37.refs_1_ = bf16[256,768]{1,0:T(8,128)(2,1)S(1)} collective-permute-done((bf16[256,768]{1,0:T(8,128)(2,1)S(1)}, bf16[256,768]{1,0:T(8,128)(2,1)S(1)}, u32[]{:S(2)}, u32[]{:S(2)}) %collective-permute-start.37) | collective-permute-done | bytes 393248 | tf_op jit(solution)/shard_map/ppermute | solution.py:608
  165.7 4.4 %collective-permute-done.45.refs_1_ = bf16[256,768]{1,0:T(8,128)(2,1)S(1)} collective-permute-done((bf16[256,768]{1,0:T(8,128)(2,1)S(1)}, bf16[256,768]{1,0:T(8,128)(2,1)S(1)}, u32[]{:S(2)}, u32[]{:S(2)}) %collective-permute-start.45) | collective-permute-done | bytes 393248 | tf_op jit(solution)/shard_map/ppermute | solution.py:611
  170.3 2.6 %collective-permute-start.51 = (bf16[256,640]{1,0:T(8,128)(2,1)S(1)}, bf16[256,640]{1,0:T(8,128)(2,1)S(1)}, u32[]{:S(2)}, u32[]{:S(2)}) collective-permute-start(bf16[256,640]{1,0:T(8,128)(2,1)S(1)} %half_add.31), channel_id=1, source_target_pairs={{0,96},{32,64},{64,32},{96,0},{1,97},{33,65},{65,33},{97,1},{2,98}... | collective-permute-start | bytes 983048 | tf_op jit(solution)/shard_map/ppermute | solution.py:611
  173.3 2.6 %collective-permute-start.34 = (bf16[128,896]{1,0:T(8,128)(2,1)S(1)}, bf16[128,896]{1,0:T(8,128)(2,1)S(1)}, u32[]{:S(2)}, u32[]{:S(2)}) collective-permute-start(bf16[128,896]{1,0:T(8,128)(2,1)S(1)} %get-tuple-element.116), channel_id=1, source_target_pairs={{0,24},{8,16},{16,8},{24,0},{1,25},{9,17},{17,9},{25,1},{2,26},{10... | collective-permute-start | bytes 688136 | tf_op jit(solution)/shard_map/ppermute | solution.py:614
  176.3 5.9 %collective-permute-done.22.refs_1_ = bf16[512,384]{1,0:T(8,128)(2,1)S(1)} collective-permute-done((bf16[512,384]{1,0:T(8,128)(2,1)S(1)}, bf16[512,384]{1,0:T(8,128)(2,1)S(1)}, u32[]{:S(2)}, u32[]{:S(2)}) %collective-permute-start.22) | collective-permute-done | bytes 393248 | tf_op jit(solution)/shard_map/ppermute | solution.py:484
  182.3 2.6 %collective-permute-start.46 = (bf16[128,768]{1,0:T(8,128)(2,1)S(1)}, bf16[128,768]{1,0:T(8,128)(2,1)S(1)}, u32[]{:S(2)}, u32[]{:S(2)}) collective-permute-start(bf16[128,768]{1,0:T(8,128)(2,1)S(1)} %get-tuple-element.130), channel_id=1, source_target_pairs={{0,96},{32,64},{64,32},{96,0},{1,97},{33,65},{65,33},{97,1},{2,98}... | collective-permute-start | bytes 589832 | tf_op jit(solution)/shard_map/ppermute | solution.py:614
  190.7 4.7 %collective-permute-done.25.right = f32[48,256]{1,0:T(8,128)S(1)} collective-permute-done((f32[48,256]{1,0:T(8,128)S(1)}, f32[48,256]{1,0:T(8,128)S(1)}, u32[]{:S(2)}, u32[]{:S(2)}) %collective-permute-start.25) | collective-permute-done | bytes 49184 | tf_op jit(solution)/shard_map/ppermute | solution.py:99
  199.5 2.7 %collective-permute-start.27 = (f32[48,256]{1,0:T(8,128)S(1)}, f32[48,256]{1,0:T(8,128)S(1)}, u32[]{:S(2)}, u32[]{:S(2)}) collective-permute-start(f32[48,256]{1,0:T(8,128)S(1)} %pair_added.5.mine), channel_id=1, source_target_pairs={{0,24},{8,16},{16,8},{24,0},{1,25},{9,17},{17,9},{25,1},{2,26},{10... | collective-permute-start | bytes 147464 | tf_op jit(solution)/shard_map/ppermute | solution.py:99
  (121 shorter events, 64.7 us)
Async XLA Ops:
  1.9 20.6 %collective-permute-start.6 = (bf16[768,256]{1,0:T(8,128)(2,1)S(1)}, bf16[768,256]{1,0:T(8,128)(2,1)S(1)}, u32[]{:S(2)}, u32[]{:S(2)}) collective-permute-start(bf16[768,256]{1,0:T(8,128)(2,1)S(1)} %get-tuple-element.76.refs_0_), channel_id=1, source_target_pairs={{0,6},{2,0},{4,2},{6,4},{1,7},{3,1},{5,3},{7,5},{8,14},{10,8},{12,... | collective-permute-start | bytes 1179656 | tf_op jit(solution)/shard_map/ppermute | solution.py:66
  2.7 19.8 %collective-permute-start.7 = (bf16[768,256]{1,0:T(8,128)(2,1)S(1)}, bf16[768,256]{1,0:T(8,128)(2,1)S(1)}, u32[]{:S(2)}, u32[]{:S(2)}) collective-permute-start(bf16[768,256]{1,0:T(8,128)(2,1)S(1)} %get-tuple-element.76.refs_0_), channel_id=1, source_target_pairs={{0,4},{2,6},{4,0},{6,2},{1,5},{3,7},{5,1},{7,3},{8,12},{10,14},{12... | collective-permute-start | bytes 1179656 | tf_op jit(solution)/shard_map/ppermute | solution.py:66
  3.5 23.3 %collective-permute-start.8 = (bf16[768,256]{1,0:T(8,128)(2,1)S(1)}, bf16[768,256]{1,0:T(8,128)(2,1)S(1)}, u32[]{:S(2)}, u32[]{:S(2)}) collective-permute-start(bf16[768,256]{1,0:T(8,128)(2,1)S(1)} %get-tuple-element.76.refs_0_), channel_id=1, source_target_pairs={{0,2},{2,4},{4,6},{6,0},{1,3},{3,5},{5,7},{7,1},{8,10},{10,12},{12... | collective-permute-start | bytes 1179656 | tf_op jit(solution)/shard_map/ppermute | solution.py:66
  7.7 15.2 %collective-permute-start.1 = (f32[48,256]{1,0:T(8,128)S(1)}, f32[48,256]{1,0:T(8,128)S(1)}, u32[]{:S(2)}, u32[]{:S(2)}) collective-permute-start(f32[48,256]{1,0:T(8,128)S(1)} %get-tuple-element.74.refs_0_), channel_id=1, source_target_pairs={{0,96},{32,0},{64,32},{96,64},{1,97},{33,1},{65,33},{97,65},{2,98}... | collective-permute-start | bytes 147464 | tf_op jit(solution)/shard_map/ppermute | solution.py:113
  11.9 47.1 %collective-permute-start.9 = (bf16[768,256]{1,0:T(8,128)(2,1)S(1)}, bf16[768,256]{1,0:T(8,128)(2,1)S(1)}, u32[]{:S(2)}, u32[]{:S(2)}) collective-permute-start(bf16[768,256]{1,0:T(8,128)(2,1)S(1)} %get-tuple-element.76.refs_0_), channel_id=1, source_target_pairs={{0,1},{1,0},{2,3},{3,2},{4,5},{5,4},{6,7},{7,6},{8,9},{9,8},{10,11... | collective-permute-start | bytes 1179656 | tf_op jit(solution)/shard_map/ppermute | solution.py:70
  22.4 37.1 %collective-permute-start.10 = (bf16[768,256]{1,0:T(8,128)(2,1)S(1)}, bf16[768,256]{1,0:T(8,128)(2,1)S(1)}, u32[]{:S(2)}, u32[]{:S(2)}) collective-permute-start(bf16[768,256]{1,0:T(8,128)(2,1)S(1)} %collective-permute-done.6.refs_1_), channel_id=1, source_target_pairs={{0,1},{1,0},{2,3},{3,2},{4,5},{5,4},{6,7},{7,6},{8,9},{9,8},{10,11... | collective-permute-start | bytes 1179656 | tf_op jit(solution)/shard_map/ppermute | solution.py:70
  22.5 37.2 %collective-permute-start.11 = (bf16[768,256]{1,0:T(8,128)(2,1)S(1)}, bf16[768,256]{1,0:T(8,128)(2,1)S(1)}, u32[]{:S(2)}, u32[]{:S(2)}) collective-permute-start(bf16[768,256]{1,0:T(8,128)(2,1)S(1)} %collective-permute-done.7.refs_2_), channel_id=1, source_target_pairs={{0,1},{1,0},{2,3},{3,2},{4,5},{5,4},{6,7},{7,6},{8,9},{9,8},{10,11... | collective-permute-start | bytes 1179656 | tf_op jit(solution)/shard_map/ppermute | solution.py:70
  26.8 39.0 %collective-permute-start.12 = (bf16[768,256]{1,0:T(8,128)(2,1)S(1)}, bf16[768,256]{1,0:T(8,128)(2,1)S(1)}, u32[]{:S(2)}, u32[]{:S(2)}) collective-permute-start(bf16[768,256]{1,0:T(8,128)(2,1)S(1)} %collective-permute-done.8.refs_3_), channel_id=1, source_target_pairs={{0,1},{1,0},{2,3},{3,2},{4,5},{5,4},{6,7},{7,6},{8,9},{9,8},{10,11... | collective-permute-start | bytes 1179656 | tf_op jit(solution)/shard_map/ppermute | solution.py:70
  72.2 27.4 %collective-permute-start.48 = (bf16[512,640]{1,0:T(8,128)(2,1)S(1)}, bf16[512,640]{1,0:T(8,128)(2,1)S(1)}, u32[]{:S(2)}, u32[]{:S(2)}) collective-permute-start(bf16[512,640]{1,0:T(8,128)(2,1)S(1)} %get-tuple-element.133), channel_id=1, source_target_pairs={{0,24},{8,16},{16,8},{24,0},{1,25},{9,17},{17,9},{25,1},{2,26},{10... | collective-permute-start | bytes 1966088 | tf_op jit(solution)/shard_map/ppermute | solution.py:604
  78.9 27.1 %collective-permute-start.42 = (bf16[512,768]{1,0:T(8,128)(2,1)S(1)}, bf16[512,768]{1,0:T(8,128)(2,1)S(1)}, u32[]{:S(2)}, u32[]{:S(2)}) collective-permute-start(bf16[512,768]{1,0:T(8,128)(2,1)S(1)} %get-tuple-element.126), channel_id=1, source_target_pairs={{0,8},{8,0},{16,24},{24,16},{1,9},{9,1},{17,25},{25,17},{2,10},{10... | collective-permute-start | bytes 2359304 | tf_op jit(solution)/shard_map/ppermute | solution.py:604
  79.0 36.1 %collective-permute-start.41 = (bf16[512,768]{1,0:T(8,128)(2,1)S(1)}, bf16[512,768]{1,0:T(8,128)(2,1)S(1)}, u32[]{:S(2)}, u32[]{:S(2)}) collective-permute-start(bf16[512,768]{1,0:T(8,128)(2,1)S(1)} %get-tuple-element.125), channel_id=1, source_target_pairs={{0,8},{8,0},{16,24},{24,16},{1,9},{9,1},{17,25},{25,17},{2,10},{10... | collective-permute-start | bytes 2359304 | tf_op jit(solution)/shard_map/ppermute | solution.py:605
  81.0 23.4 %collective-permute-start.47 = (bf16[512,640]{1,0:T(8,128)(2,1)S(1)}, bf16[512,640]{1,0:T(8,128)(2,1)S(1)}, u32[]{:S(2)}, u32[]{:S(2)}) collective-permute-start(bf16[512,640]{1,0:T(8,128)(2,1)S(1)} %get-tuple-element.132), channel_id=1, source_target_pairs={{0,24},{8,16},{16,8},{24,0},{1,25},{9,17},{17,9},{25,1},{2,26},{10... | collective-permute-start | bytes 1966088 | tf_op jit(solution)/shard_map/ppermute | solution.py:605
  81.5 17.8 %collective-permute-start.29 = (bf16[1024,128]{1,0:T(8,128)(2,1)S(1)}, bf16[1024,128]{1,0:T(8,128)(2,1)S(1)}, u32[]{:S(2)}, u32[]{:S(2)}) collective-permute-start(bf16[1024,128]{1,0:T(8,128)(2,1)S(1)} %get-tuple-element.111), channel_id=1, source_target_pairs={{0,32},{32,0},{64,96},{96,64},{1,33},{33,1},{65,97},{97,65},{2,34}... | collective-permute-start | bytes 786440 | tf_op jit(solution)/shard_map/ppermute | solution.py:603
  99.3 55.5 %collective-permute-start.20 = (bf16[8,256,384]{2,1,0:T(8,128)(2,1)S(1)}, bf16[8,256,384]{2,1,0:T(8,128)(2,1)S(1)}, u32[]{:S(2)}, u32[]{:S(2)}) collective-permute-start(bf16[8,256,384]{2,1,0:T(8,128)(2,1)S(1)} %get-tuple-element.97), channel_id=1, source_target_pairs={{0,1},{1,0},{2,3},{3,2},{4,5},{5,4},{6,7},{7,6},{8,9},{9,8},{10,11... | collective-permute-start | bytes 4718600 | tf_op jit(solution)/shard_map/ppermute | solution.py:471
  99.6 21.7 %collective-permute-start.36 = (bf16[512,768]{1,0:T(8,128)(2,1)S(1)}, bf16[512,768]{1,0:T(8,128)(2,1)S(1)}, u32[]{:S(2)}, u32[]{:S(2)}) collective-permute-start(bf16[512,768]{1,0:T(8,128)(2,1)S(1)} %get-tuple-element.119), channel_id=1, source_target_pairs={{0,96},{32,64},{64,32},{96,0},{1,97},{33,65},{65,33},{97,1},{2,98}... | collective-permute-start | bytes 2359304 | tf_op jit(solution)/shard_map/ppermute | solution.py:604
  104.4 20.4 %collective-permute-start.30 = (bf16[512,768]{1,0:T(8,128)(2,1)S(1)}, bf16[512,768]{1,0:T(8,128)(2,1)S(1)}, u32[]{:S(2)}, u32[]{:S(2)}) collective-permute-start(bf16[512,768]{1,0:T(8,128)(2,1)S(1)} %get-tuple-element.112), channel_id=1, source_target_pairs={{0,32},{32,0},{64,96},{96,64},{1,33},{33,1},{65,97},{97,65},{2,34}... | collective-permute-start | bytes 2359304 | tf_op jit(solution)/shard_map/ppermute | solution.py:604
  106.0 31.6 %collective-permute-start.35 = (bf16[512,768]{1,0:T(8,128)(2,1)S(1)}, bf16[512,768]{1,0:T(8,128)(2,1)S(1)}, u32[]{:S(2)}, u32[]{:S(2)}) collective-permute-start(bf16[512,768]{1,0:T(8,128)(2,1)S(1)} %get-tuple-element.118), channel_id=1, source_target_pairs={{0,96},{32,64},{64,32},{96,0},{1,97},{33,65},{65,33},{97,1},{2,98}... | collective-permute-start | bytes 2359304 | tf_op jit(solution)/shard_map/ppermute | solution.py:605
  115.1 25.0 %collective-permute-start.28 = (bf16[512,768]{1,0:T(8,128)(2,1)S(1)}, bf16[512,768]{1,0:T(8,128)(2,1)S(1)}, u32[]{:S(2)}, u32[]{:S(2)}) collective-permute-start(bf16[512,768]{1,0:T(8,128)(2,1)S(1)} %get-tuple-element.109), channel_id=1, source_target_pairs={{0,32},{32,0},{64,96},{96,64},{1,33},{33,1},{65,97},{97,65},{2,34}... | collective-permute-start | bytes 2359304 | tf_op jit(solution)/shard_map/ppermute | solution.py:605
  121.3 21.8 %collective-permute-start.50 = (bf16[256,640]{1,0:T(8,128)(2,1)S(1)}, bf16[256,640]{1,0:T(8,128)(2,1)S(1)}, u32[]{:S(2)}, u32[]{:S(2)}) collective-permute-start(bf16[256,640]{1,0:T(8,128)(2,1)S(1)} %get-tuple-element.135), channel_id=1, source_target_pairs={{0,8},{8,0},{16,24},{24,16},{1,9},{9,1},{17,25},{25,17},{2,10},{10... | collective-permute-start | bytes 983048 | tf_op jit(solution)/shard_map/ppermute | solution.py:607
  124.8 19.7 %collective-permute-start.44 = (bf16[256,768]{1,0:T(8,128)(2,1)S(1)}, bf16[256,768]{1,0:T(8,128)(2,1)S(1)}, u32[]{:S(2)}, u32[]{:S(2)}) collective-permute-start(bf16[256,768]{1,0:T(8,128)(2,1)S(1)} %get-tuple-element.128), channel_id=1, source_target_pairs={{0,24},{8,16},{16,8},{24,0},{1,25},{9,17},{17,9},{25,1},{2,26},{10... | collective-permute-start | bytes 1179656 | tf_op jit(solution)/shard_map/ppermute | solution.py:607
  144.5 20.3 %collective-permute-start.31 = (bf16[256,896]{1,0:T(8,128)(2,1)S(1)}, bf16[256,896]{1,0:T(8,128)(2,1)S(1)}, u32[]{:S(2)}, u32[]{:S(2)}) collective-permute-start(bf16[256,896]{1,0:T(8,128)(2,1)S(1)} %get-tuple-element.113), channel_id=1, source_target_pairs={{0,96},{32,64},{64,32},{96,0},{1,97},{33,65},{65,33},{97,1},{2,98}... | collective-permute-start | bytes 1376264 | tf_op jit(solution)/shard_map/ppermute | solution.py:608
  152.4 17.6 %collective-permute-start.45 = (bf16[256,768]{1,0:T(8,128)(2,1)S(1)}, bf16[256,768]{1,0:T(8,128)(2,1)S(1)}, u32[]{:S(2)}, u32[]{:S(2)}) collective-permute-start(bf16[256,768]{1,0:T(8,128)(2,1)S(1)} %half_add.27), channel_id=1, source_target_pairs={{0,32},{32,0},{64,96},{96,64},{1,33},{33,1},{65,97},{97,65},{2,34}... | collective-permute-start | bytes 1179656 | tf_op jit(solution)/shard_map/ppermute | solution.py:611
  154.4 15.9 %collective-permute-start.33 = (bf16[256,896]{1,0:T(8,128)(2,1)S(1)}, bf16[256,896]{1,0:T(8,128)(2,1)S(1)}, u32[]{:S(2)}, u32[]{:S(2)}) collective-permute-start(bf16[256,896]{1,0:T(8,128)(2,1)S(1)} %half_add.19), channel_id=1, source_target_pairs={{0,8},{8,0},{16,24},{24,16},{1,9},{9,1},{17,25},{25,17},{2,10},{10... | collective-permute-start | bytes 1376264 | tf_op jit(solution)/shard_map/ppermute | solution.py:611
  154.8 15.3 %collective-permute-start.39 = (bf16[256,768]{1,0:T(8,128)(2,1)S(1)}, bf16[256,768]{1,0:T(8,128)(2,1)S(1)}, u32[]{:S(2)}, u32[]{:S(2)}) collective-permute-start(bf16[256,768]{1,0:T(8,128)(2,1)S(1)} %half_add.23), channel_id=1, source_target_pairs={{0,24},{8,16},{16,8},{24,0},{1,25},{9,17},{17,9},{25,1},{2,26},{10... | collective-permute-start | bytes 1179656 | tf_op jit(solution)/shard_map/ppermute | solution.py:611
  164.8 17.4 %collective-permute-start.22 = (bf16[512,384]{1,0:T(8,128)(2,1)S(1)}, bf16[512,384]{1,0:T(8,128)(2,1)S(1)}, u32[]{:S(2)}, u32[]{:S(2)}) collective-permute-start(bf16[512,384]{1,0:T(8,128)(2,1)S(1)} %get-tuple-element.100), channel_id=1, source_target_pairs={{0,6},{2,0},{4,2},{6,4},{1,7},{3,1},{5,3},{7,5},{8,14},{10,8},{12,... | collective-permute-start | bytes 1179656 | tf_op jit(solution)/shard_map/ppermute | solution.py:484
  170.1 14.8 %collective-permute-start.23 = (bf16[512,384]{1,0:T(8,128)(2,1)S(1)}, bf16[512,384]{1,0:T(8,128)(2,1)S(1)}, u32[]{:S(2)}, u32[]{:S(2)}) collective-permute-start(bf16[512,384]{1,0:T(8,128)(2,1)S(1)} %get-tuple-element.101), channel_id=1, source_target_pairs={{0,4},{2,6},{4,0},{6,2},{1,5},{3,7},{5,1},{7,3},{8,12},{10,14},{12... | collective-permute-start | bytes 1179656 | tf_op jit(solution)/shard_map/ppermute | solution.py:484
  170.1 15.7 %collective-permute-start.49 = (bf16[256,640]{1,0:T(8,128)(2,1)S(1)}, bf16[256,640]{1,0:T(8,128)(2,1)S(1)}, u32[]{:S(2)}, u32[]{:S(2)}) collective-permute-start(bf16[256,640]{1,0:T(8,128)(2,1)S(1)} %get-tuple-element.134), channel_id=1, source_target_pairs={{0,8},{8,0},{16,24},{24,16},{1,9},{9,1},{17,25},{25,17},{2,10},{10... | collective-permute-start | bytes 983048 | tf_op jit(solution)/shard_map/ppermute | solution.py:608
  170.3 15.6 %collective-permute-start.51 = (bf16[256,640]{1,0:T(8,128)(2,1)S(1)}, bf16[256,640]{1,0:T(8,128)(2,1)S(1)}, u32[]{:S(2)}, u32[]{:S(2)}) collective-permute-start(bf16[256,640]{1,0:T(8,128)(2,1)S(1)} %half_add.31), channel_id=1, source_target_pairs={{0,96},{32,64},{64,32},{96,0},{1,97},{33,65},{65,33},{97,1},{2,98}... | collective-permute-start | bytes 983048 | tf_op jit(solution)/shard_map/ppermute | solution.py:611
  173.3 29.0 %collective-permute-start.34 = (bf16[128,896]{1,0:T(8,128)(2,1)S(1)}, bf16[128,896]{1,0:T(8,128)(2,1)S(1)}, u32[]{:S(2)}, u32[]{:S(2)}) collective-permute-start(bf16[128,896]{1,0:T(8,128)(2,1)S(1)} %get-tuple-element.116), channel_id=1, source_target_pairs={{0,24},{8,16},{16,8},{24,0},{1,25},{9,17},{17,9},{25,1},{2,26},{10... | collective-permute-start | bytes 688136 | tf_op jit(solution)/shard_map/ppermute | solution.py:614
  182.3 19.9 %collective-permute-start.46 = (bf16[128,768]{1,0:T(8,128)(2,1)S(1)}, bf16[128,768]{1,0:T(8,128)(2,1)S(1)}, u32[]{:S(2)}, u32[]{:S(2)}) collective-permute-start(bf16[128,768]{1,0:T(8,128)(2,1)S(1)} %get-tuple-element.130), channel_id=1, source_target_pairs={{0,96},{32,64},{64,32},{96,0},{1,97},{33,65},{65,33},{97,1},{2,98}... | collective-permute-start | bytes 589832 | tf_op jit(solution)/shard_map/ppermute | solution.py:614
  184.9 17.3 %collective-permute-start.40 = (bf16[128,768]{1,0:T(8,128)(2,1)S(1)}, bf16[128,768]{1,0:T(8,128)(2,1)S(1)}, u32[]{:S(2)}, u32[]{:S(2)}) collective-permute-start(bf16[128,768]{1,0:T(8,128)(2,1)S(1)} %get-tuple-element.123), channel_id=1, source_target_pairs={{0,8},{8,0},{16,24},{24,16},{1,9},{9,1},{17,25},{25,17},{2,10},{10... | collective-permute-start | bytes 589832 | tf_op jit(solution)/shard_map/ppermute | solution.py:614
  186.1 16.1 %collective-permute-start.52 = (bf16[128,640]{1,0:T(8,128)(2,1)S(1)}, bf16[128,640]{1,0:T(8,128)(2,1)S(1)}, u32[]{:S(2)}, u32[]{:S(2)}) collective-permute-start(bf16[128,640]{1,0:T(8,128)(2,1)S(1)} %get-tuple-element.137), channel_id=1, source_target_pairs={{0,32},{32,0},{64,96},{96,64},{1,33},{33,1},{65,97},{97,65},{2,34}... | collective-permute-start | bytes 491528 | tf_op jit(solution)/shard_map/ppermute | solution.py:614
  (24 other events, 163.5 us)
where the time goes:
time: 207 us; the launch traced here: 206 us
  waiting for transfers between devices  95.2 us (46%)
  starting transfers between devices  68.9 us (33%)
  Pallas kernels  41.2 us (20%)
    ppermute x6, waiting for transfers between devices, gathered(): near.append(lax.ppermute(x, 'y', shift(-k)))  25.3 us
    ppermute x4, waiting for transfers between devices, body(): came_b = lax.ppermute(send_b, major, pair[0])  18.6 us
    pallas_call x4, Pallas kernels, hidden_part(): pl.pallas_call(hidden_kernel(p, lent), grid=(1,), out_shape=tuple((jax.Sh...  15.2 us
    ppermute x6, waiting for transfers between devices, ring_pieces(): came.append(lax.ppermute(x, axis, shift(k)))  14.3 us
    ppermute x6, starting transfers between devices, ring_pieces(): came.append(lax.ppermute(x, axis, shift(k)))  12.8 us
    ppermute x4, waiting for transfers between devices, body(): next_b = lax.ppermute(send_b, major, pair[1])  10.2 us
    pallas_call x1, Pallas kernels, back(): pl.pallas_call(back_kernel, in_specs=[smem_spec()] + [vmem_spec()] * (3 *...  8.74 us
    ppermute x4, waiting for transfers between devices, tok_halves(): came = lax.ppermute(x, axis, pairs)  8.56 us
  transfers between devices with their start and end apart: 53, of which 21 were waited for; matrix products, arithmetic and copies ran while one was open for 0% of the time, Pallas kernels for 16%

commit v1 on v0

--- a/solution.py
+++ b/solution.py
@@ -245,22 +245,6 @@
         normed = tokens[rows, :].astype(f32) * scale
         inner = gain_row * grad[rows, :] - normed * acc[row, :]
         out[rows, :] = (cotangent[rows, :].astype(f32) + scale * inner).astype(bf16)
-
-
-def input_grads(groups, coords, tokens, cotangent, gain, table, grad, mine, came):
-    rows, feat = tokens.shape
-    return pl.pallas_call(
-        input_kernel,
-        out_shape=(
-            jax.ShapeDtypeStruct((rows, feat), bf16),
-            jax.ShapeDtypeStruct((1, feat), f32),
-        ),
-        in_specs=[smem_spec(), smem_spec()] + [vmem_spec()] * 7,
-        out_specs=(vmem_spec(),) * 2,
-        scratch_shapes=[pltpu.VMEM(table.shape, f32)],
-        compiler_params=limits(6),
-        name="input_grads",
-    )(in_hbm(groups), coords, tokens, cotangent, gain, table, grad, mine, came)
 
 
 def branch_kernel(tokens, running, quad, own, *refs):
@@ -550,26 +534,44 @@
 
 
 def finish_kernel(*refs):
-    ins, outs = refs[: 2 * RING], refs[2 * RING :]
+    inputs, ins = refs[:9], refs[9 : 9 + 2 * RING]
+    out, grad_gain, *outs, acc = refs[9 + 2 * RING :]
+    input_kernel(*inputs, out, grad_gain, acc)
     for p, runs in enumerate(sections(outs[0].shape[1] // RING)):
         total = ins[2 * p][...].astype(f32) + ins[2 * p + 1][...].astype(f32)
         first = 0
-        for out, column, width in runs:
-            outs[out][:, column : column + width] = total[:, first : first + width]
+        for i, column, width in runs:
+            outs[i][:, column : column + width] = total[:, first : first + width]
             first += width
 
 
-def finished(pairs, width):
-    rows = pairs[0][0].shape[0]
-    out = jax.ShapeDtypeStruct((rows, width), f32)
+def finished(groups, coords, tokens, cotangent, gain, table, grad, mine, came, pairs, width):
+    rows, feat = tokens.shape
+    out = jax.ShapeDtypeStruct((pairs[0][0].shape[0], width), f32)
     return pl.pallas_call(
         finish_kernel,
-        out_shape=(out,) * 3,
-        in_specs=[vmem_spec()] * (2 * RING),
-        out_specs=(vmem_spec(),) * 3,
-        compiler_params=limits(6),
+        out_shape=(
+            jax.ShapeDtypeStruct((rows, feat), bf16),
+            jax.ShapeDtypeStruct((1, feat), f32),
+        )
+        + (out,) * 3,
+        in_specs=[smem_spec(), smem_spec()] + [vmem_spec()] * (7 + 2 * RING),
+        out_specs=(vmem_spec(),) * 5,
+        scratch_shapes=[pltpu.VMEM(table.shape, f32)],
+        compiler_params=limits(12),
         name="finished",
-    )(*[a for pair in pairs for a in pair])
+    )(
+        in_hbm(groups),
+        coords,
+        tokens,
+        cotangent,
+        gain,
+        table,
+        grad,
+        mine,
+        came,
+        *[a for pair in pairs for a in pair],
+    )
 
 
 def body(tokens, norm_gain, running_sq, gate_weight, up_weight, down_weight_t, groups, cotangent):
@@ -613,8 +615,6 @@
         send, keep = split_add(keep, came)
         came = lax.ppermute(send, minor, pair[1])
         last.append((keep, came))
-    grad_down_t, grad_gate, grad_up = finished(last, gate_weight.shape[1])
-
     far, near = back(
         coords,
         [[q[1] for q in parts], [q[2] for q in parts], [q[0] for q in parts]],
@@ -623,9 +623,10 @@
     kept, came_y = mp_scattered(far, near)
     grad, local = partials(groups, tokens, table, kept, came_y)
     mine, came = tok_halves(local)
-    grad_tokens, grad_gain = input_grads(groups, coords, tokens, cotangent, gain, table, grad, mine, came)
-
     block_out, running_new = branch_out(tokens, running_sq.reshape(1, feat), quad, kept, came_y)
+    grad_tokens, grad_gain, grad_down_t, grad_gate, grad_up = finished(
+        groups, coords, tokens, cotangent, gain, table, grad, mine, came, last, gate_weight.shape[1]
+    )
     return (
         block_out,
         grad_tokens,

time: 207 us -> 206 us (level)
  the two profiles are of different devices: /device:TPU:24 before, /device:TPU:30 now
where the time goes in v1:
time: 206 us
  waiting for transfers between devices  108 us (52%)
  starting transfers between devices  56 us (27%)
  Pallas kernels  40.5 us (20%)
    ppermute x6, waiting for transfers between devices, gathered(): near.append(lax.ppermute(x, 'y', shift(-k)))  25.3 us
    ppermute x4, waiting for transfers between devices, body(): came_b = lax.ppermute(send_b, major, pair[0])  18.6 us
    ppermute x6, waiting for transfers between devices, ring_pieces(): came.append(lax.ppermute(x, axis, shift(k)))  17.6 us
    pallas_call x4, Pallas kernels, hidden_part(): pl.pallas_call(hidden_kernel(p, lent), grid=(1,), out_shape=tuple((jax.Sh...  15.2 us
    ppermute x4, waiting for transfers between devices, body(): next_b = lax.ppermute(send_b, major, pair[1])  14.3 us
    ppermute x4, waiting for transfers between devices, tok_halves(): came = lax.ppermute(x, axis, pairs)  13.6 us
    ppermute x4, waiting for transfers between devices, body(): came_a = lax.ppermute(send_a, major, pair[0])  10.1 us
    ppermute x6, starting transfers between devices, ring_pieces(): came.append(lax.ppermute(x, axis, shift(k)))  9.49 us
  transfers between devices with their start and end apart: 53, of which 22 were waited for; matrix products, arithmetic and copies ran while one was open for 0% of the time, Pallas kernels for 16%

profile of v1, /device:TPU:30, one launch (start us, length us, event | category | flops | bytes accessed | tf_op | source)
XLA Modules:
  0.0 205.8 jit_solution(11754481837483100275)
XLA Ops:
  11.9 10.5 %collective-permute-done.6.refs_1_ = bf16[768,256]{1,0:T(8,128)(2,1)S(1)} collective-permute-done((bf16[768,256]{1,0:T(8,128)(2,1)S(1)}, bf16[768,256]{1,0:T(8,128)(2,1)S(1)}, u32[]{:S(2)}, u32[]{:S(2)}) %collective-permute-start.6) | collective-permute-done | bytes 393248 | tf_op jit(solution)/shard_map/ppermute | solution.py:66
  23.0 3.9 %collective-permute-start.2 = (f32[48,256]{1,0:T(8,128)S(1)}, f32[48,256]{1,0:T(8,128)S(1)}, u32[]{:S(2)}, u32[]{:S(2)}) collective-permute-start(f32[48,256]{1,0:T(8,128)S(1)} %get-tuple-element.74.refs_0_), channel_id=1, source_target_pairs={{0,64},{32,96},{64,0},{96,32},{1,65},{33,97},{65,1},{97,33},{2,66}... | collective-permute-start | bytes 147464 | tf_op jit(solution)/shard_map/ppermute | solution.py:113
  29.5 3.6 %collective-permute-done.3.b = f32[48,256]{1,0:T(8,128)S(1)} collective-permute-done((f32[48,256]{1,0:T(8,128)S(1)}, f32[48,256]{1,0:T(8,128)S(1)}, u32[]{:S(2)}, u32[]{:S(2)}) %collective-permute-start.3) | collective-permute-done | bytes 49184 | tf_op jit(solution)/shard_map/ppermute | solution.py:113
  33.9 4.5 %collective-permute-done.4.c = f32[48,256]{1,0:T(8,128)S(1)} collective-permute-done((f32[48,256]{1,0:T(8,128)S(1)}, f32[48,256]{1,0:T(8,128)S(1)}, u32[]{:S(2)}, u32[]{:S(2)}) %collective-permute-start.4) | collective-permute-done | bytes 49184 | tf_op jit(solution)/shard_map/ppermute | solution.py:113
  38.6 5.4 %collective-permute-done.5.d = f32[48,256]{1,0:T(8,128)S(1)} collective-permute-done((f32[48,256]{1,0:T(8,128)S(1)}, f32[48,256]{1,0:T(8,128)S(1)}, u32[]{:S(2)}, u32[]{:S(2)}) %collective-permute-start.5) | collective-permute-done | bytes 49184 | tf_op jit(solution)/shard_map/ppermute | solution.py:113
  44.1 5.3 %collective-permute-done.13.refs_9_ = f32[48,256]{1,0:T(8,128)S(1)} collective-permute-done((f32[48,256]{1,0:T(8,128)S(1)}, f32[48,256]{1,0:T(8,128)S(1)}, u32[]{:S(2)}, u32[]{:S(2)}) %collective-permute-start.13) | collective-permute-done | bytes 49184 | tf_op jit(solution)/shard_map/ppermute | solution.py:66
  49.6 5.4 %collective-permute-done.14.refs_10_ = f32[48,256]{1,0:T(8,128)S(1)} collective-permute-done((f32[48,256]{1,0:T(8,128)S(1)}, f32[48,256]{1,0:T(8,128)S(1)}, u32[]{:S(2)}, u32[]{:S(2)}) %collective-permute-start.14) | collective-permute-done | bytes 49184 | tf_op jit(solution)/shard_map/ppermute | solution.py:66
  55.0 4.1 %collective-permute-done.15.refs_11_ = f32[48,256]{1,0:T(8,128)S(1)} collective-permute-done((f32[48,256]{1,0:T(8,128)S(1)}, f32[48,256]{1,0:T(8,128)S(1)}, u32[]{:S(2)}, u32[]{:S(2)}) %collective-permute-start.15) | collective-permute-done | bytes 49184 | tf_op jit(solution)/shard_map/ppermute | solution.py:66
  62.3 3.5 %staged.2 = (bf16[2048,1024]{1,0:T(8,128)(2,1)S(1)}, bf16[2048,1024]{1,0:T(8,128)(2,1)S(1)}) custom-call(bf16[2048,1024]{1,0:T(8,128)(2,1)} %refs_0_.3, bf16[2048,1024]{1,0:T(8,128)(2,1)} %refs_1_.1), custom_call_target="tpu_custom_call" | custom-call | tf_op jit(solution)/shard_map/staged/pallas_call | solution.py:151
  68.1 4.0 %hidden_part.7 = (bf16[256,384]{1,0:T(8,128)(2,1)S(1)}, bf16[256,384]{1,0:T(8,128)(2,1)S(1)}, bf16[256,384]{1,0:T(8,128)(2,1)S(1)}, bf16[512,640]{1,0:T(8,128)(2...) custom-call(s32[4]{0:T(128)S(1)} %pad_add_fusion.coords.refs_1_, ...), custom_call_target="tpu_custom_call" | custom-call | tf_op jit(solution)/shard_map/hidden_part/pallas_call | solution.py:385
  72.9 3.7 %hidden_part.6 = (bf16[256,384]{1,0:T(8,128)(2,1)S(1)}, bf16[256,384]{1,0:T(8,128)(2,1)S(1)}, bf16[256,384]{1,0:T(8,128)(2,1)S(1)}, bf16[512,768]{1,0:T(8,128)(2...) custom-call(s32[4]{0:T(128)S(1)} %pad_add_fusion.coords.refs_1_, ...), custom_call_target="tpu_custom_call" | custom-call | tf_op jit(solution)/shard_map/hidden_part/pallas_call | solution.py:385
  78.7 2.8 %collective-permute-start.47 = (bf16[512,640]{1,0:T(8,128)(2,1)S(1)}, bf16[512,640]{1,0:T(8,128)(2,1)S(1)}, u32[]{:S(2)}, u32[]{:S(2)}) collective-permute-start(bf16[512,640]{1,0:T(8,128)(2,1)S(1)} %get-tuple-element.129), channel_id=1, source_target_pairs={{0,24},{8,16},{16,8},{24,0},{1,25},{9,17},{17,9},{25,1},{2,26},{10... | collective-permute-start | bytes 1966088 | tf_op jit(solution)/shard_map/ppermute | solution.py:607
  83.1 3.7 %hidden_part.5 = (bf16[256,384]{1,0:T(8,128)(2,1)S(1)}, bf16[256,384]{1,0:T(8,128)(2,1)S(1)}, bf16[256,384]{1,0:T(8,128)(2,1)S(1)}, bf16[512,768]{1,0:T(8,128)(2...) custom-call(s32[4]{0:T(128)S(1)} %pad_add_fusion.coords.refs_1_, ...), custom_call_target="tpu_custom_call" | custom-call | tf_op jit(solution)/shard_map/hidden_part/pallas_call | solution.py:385
  86.8 3.7 %hidden_part.4 = (bf16[256,384]{1,0:T(8,128)(2,1)S(1)}, bf16[256,384]{1,0:T(8,128)(2,1)S(1)}, bf16[256,384]{1,0:T(8,128)(2,1)S(1)}, bf16[512,768]{1,0:T(8,128)(2...) custom-call(s32[4]{0:T(128)S(1)} %pad_add_fusion.coords.refs_1_, ...), custom_call_target="tpu_custom_call" | custom-call | tf_op jit(solution)/shard_map/hidden_part/pallas_call | solution.py:385
  90.5 8.7 %back.1 = (bf16[8,256,384]{2,1,0:T(8,128)(2,1)S(1)}, bf16[8,256,384]{2,1,0:T(8,128)(2,1)S(1)}) custom-call(s32[4]{0:T(128)S(1)} %pad_add_fusion.coords.refs_1_, bf16[256,384]{1,0:T(8,128)(2,1)S(1)} %get-tuple-element.84.refs_0_, bf16[256,384]{1,0:T(8,128)(2,1)S(1)} %get-tuple-element.85.refs_1_, bf16[256,384]{1,0:T(8,128)(2,1)S(1)} %get-tuple-element.86.refs_2_, ...), custom_call_target="tpu_custom_call" | custom-call | tf_op jit(solution)/shard_map/back/pallas_call | solution.py:433
  99.6 2.6 %collective-permute-start.36 = (bf16[512,768]{1,0:T(8,128)(2,1)S(1)}, bf16[512,768]{1,0:T(8,128)(2,1)S(1)}, u32[]{:S(2)}, u32[]{:S(2)}) collective-permute-start(bf16[512,768]{1,0:T(8,128)(2,1)S(1)} %get-tuple-element.116), channel_id=1, source_target_pairs={{0,96},{32,64},{64,32},{96,0},{1,97},{33,65},{65,33},{97,1},{2,98}... | collective-permute-start | bytes 2359304 | tf_op jit(solution)/shard_map/ppermute | solution.py:606
  106.0 2.5 %collective-permute-start.35 = (bf16[512,768]{1,0:T(8,128)(2,1)S(1)}, bf16[512,768]{1,0:T(8,128)(2,1)S(1)}, u32[]{:S(2)}, u32[]{:S(2)}) collective-permute-start(bf16[512,768]{1,0:T(8,128)(2,1)S(1)} %get-tuple-element.115), channel_id=1, source_target_pairs={{0,96},{32,64},{64,32},{96,0},{1,97},{33,65},{65,33},{97,1},{2,98}... | collective-permute-start | bytes 2359304 | tf_op jit(solution)/shard_map/ppermute | solution.py:607
  108.5 4.3 %collective-permute-done.41.refs_1_ = bf16[512,768]{1,0:T(8,128)(2,1)S(1)} collective-permute-done((bf16[512,768]{1,0:T(8,128)(2,1)S(1)}, bf16[512,768]{1,0:T(8,128)(2,1)S(1)}, u32[]{:S(2)}, u32[]{:S(2)}) %collective-permute-start.41) | collective-permute-done | bytes 786464 | tf_op jit(solution)/shard_map/ppermute | solution.py:607
  114.6 6.7 %collective-permute-done.36.refs_1_ = bf16[512,768]{1,0:T(8,128)(2,1)S(1)} collective-permute-done((bf16[512,768]{1,0:T(8,128)(2,1)S(1)}, bf16[512,768]{1,0:T(8,128)(2,1)S(1)}, u32[]{:S(2)}, u32[]{:S(2)}) %collective-permute-start.36) | collective-permute-done | bytes 786464 | tf_op jit(solution)/shard_map/ppermute | solution.py:606
  121.5 3.3 %collective-permute-done.30.refs_1_ = bf16[512,768]{1,0:T(8,128)(2,1)S(1)} collective-permute-done((bf16[512,768]{1,0:T(8,128)(2,1)S(1)}, bf16[512,768]{1,0:T(8,128)(2,1)S(1)}, u32[]{:S(2)}, u32[]{:S(2)}) %collective-permute-start.30) | collective-permute-done | bytes 786464 | tf_op jit(solution)/shard_map/ppermute | solution.py:606
  125.5 12.1 %collective-permute-done.35.refs_1_ = bf16[512,768]{1,0:T(8,128)(2,1)S(1)} collective-permute-done((bf16[512,768]{1,0:T(8,128)(2,1)S(1)}, bf16[512,768]{1,0:T(8,128)(2,1)S(1)}, u32[]{:S(2)}, u32[]{:S(2)}) %collective-permute-start.35) | collective-permute-done | bytes 786464 | tf_op jit(solution)/shard_map/ppermute | solution.py:607
  137.6 2.5 %collective-permute-start.32 = (bf16[256,896]{1,0:T(8,128)(2,1)S(1)}, bf16[256,896]{1,0:T(8,128)(2,1)S(1)}, u32[]{:S(2)}, u32[]{:S(2)}) collective-permute-start(bf16[256,896]{1,0:T(8,128)(2,1)S(1)} %get-tuple-element.111), channel_id=1, source_target_pairs={{0,96},{32,64},{64,32},{96,0},{1,97},{33,65},{65,33},{97,1},{2,98}... | collective-permute-start | bytes 1376264 | tf_op jit(solution)/shard_map/ppermute | solution.py:609
  144.8 6.8 %collective-permute-done.43.refs_1_ = bf16[256,768]{1,0:T(8,128)(2,1)S(1)} collective-permute-done((bf16[256,768]{1,0:T(8,128)(2,1)S(1)}, bf16[256,768]{1,0:T(8,128)(2,1)S(1)}, u32[]{:S(2)}, u32[]{:S(2)}) %collective-permute-start.43) | collective-permute-done | bytes 393248 | tf_op jit(solution)/shard_map/ppermute | solution.py:610
  156.1 7.5 %collective-permute-done.37.refs_1_ = bf16[256,768]{1,0:T(8,128)(2,1)S(1)} collective-permute-done((bf16[256,768]{1,0:T(8,128)(2,1)S(1)}, bf16[256,768]{1,0:T(8,128)(2,1)S(1)}, u32[]{:S(2)}, u32[]{:S(2)}) %collective-permute-start.37) | collective-permute-done | bytes 393248 | tf_op jit(solution)/shard_map/ppermute | solution.py:610
  163.6 2.7 %collective-permute-start.23 = (bf16[512,384]{1,0:T(8,128)(2,1)S(1)}, bf16[512,384]{1,0:T(8,128)(2,1)S(1)}, u32[]{:S(2)}, u32[]{:S(2)}) collective-permute-start(bf16[512,384]{1,0:T(8,128)(2,1)S(1)} %get-tuple-element.101), channel_id=1, source_target_pairs={{0,4},{2,6},{4,0},{6,2},{1,5},{3,7},{5,1},{7,3},{8,12},{10,14},{12... | collective-permute-start | bytes 1179656 | tf_op jit(solution)/shard_map/ppermute | solution.py:468
  166.6 2.9 %collective-permute-done.45.refs_1_ = bf16[256,768]{1,0:T(8,128)(2,1)S(1)} collective-permute-done((bf16[256,768]{1,0:T(8,128)(2,1)S(1)}, bf16[256,768]{1,0:T(8,128)(2,1)S(1)}, u32[]{:S(2)}, u32[]{:S(2)}) %collective-permute-start.45) | collective-permute-done | bytes 393248 | tf_op jit(solution)/shard_map/ppermute | solution.py:613
  170.8 2.7 %collective-permute-start.51 = (bf16[256,640]{1,0:T(8,128)(2,1)S(1)}, bf16[256,640]{1,0:T(8,128)(2,1)S(1)}, u32[]{:S(2)}, u32[]{:S(2)}) collective-permute-start(bf16[256,640]{1,0:T(8,128)(2,1)S(1)} %half_add.31), channel_id=1, source_target_pairs={{0,96},{32,64},{64,32},{96,0},{1,97},{33,65},{65,33},{97,1},{2,98}... | collective-permute-start | bytes 983048 | tf_op jit(solution)/shard_map/ppermute | solution.py:613
  173.7 5.6 %collective-permute-done.22.refs_1_ = bf16[512,384]{1,0:T(8,128)(2,1)S(1)} collective-permute-done((bf16[512,384]{1,0:T(8,128)(2,1)S(1)}, bf16[512,384]{1,0:T(8,128)(2,1)S(1)}, u32[]{:S(2)}, u32[]{:S(2)}) %collective-permute-start.22) | collective-permute-done | bytes 393248 | tf_op jit(solution)/shard_map/ppermute | solution.py:468
  181.1 2.7 %collective-permute-start.46 = (bf16[128,768]{1,0:T(8,128)(2,1)S(1)}, bf16[128,768]{1,0:T(8,128)(2,1)S(1)}, u32[]{:S(2)}, u32[]{:S(2)}) collective-permute-start(bf16[128,768]{1,0:T(8,128)(2,1)S(1)} %get-tuple-element.127), channel_id=1, source_target_pairs={{0,96},{32,64},{64,32},{96,0},{1,97},{33,65},{65,33},{97,1},{2,98}... | collective-permute-start | bytes 589832 | tf_op jit(solution)/shard_map/ppermute | solution.py:616
  189.6 4.6 %collective-permute-done.25.right = f32[48,256]{1,0:T(8,128)S(1)} collective-permute-done((f32[48,256]{1,0:T(8,128)S(1)}, f32[48,256]{1,0:T(8,128)S(1)}, u32[]{:S(2)}, u32[]{:S(2)}) %collective-permute-start.25) | collective-permute-done | bytes 49184 | tf_op jit(solution)/shard_map/ppermute | solution.py:99
  194.8 3.6 %collective-permute-done.26.right = f32[48,256]{1,0:T(8,128)S(1)} collective-permute-done((f32[48,256]{1,0:T(8,128)S(1)}, f32[48,256]{1,0:T(8,128)S(1)}, u32[]{:S(2)}, u32[]{:S(2)}) %collective-permute-start.26) | collective-permute-done | bytes 49184 | tf_op jit(solution)/shard_map/ppermute | solution.py:99
  200.1 3.7 %collective-permute-done.27.refs_8_ = f32[48,256]{1,0:T(8,128)S(1)} collective-permute-done((f32[48,256]{1,0:T(8,128)S(1)}, f32[48,256]{1,0:T(8,128)S(1)}, u32[]{:S(2)}, u32[]{:S(2)}) %collective-permute-start.27) | collective-permute-done | bytes 49184 | tf_op jit(solution)/shard_map/ppermute | solution.py:99
  (120 shorter events, 54.9 us)
Async XLA Ops:
  1.9 20.6 %collective-permute-start.6 = (bf16[768,256]{1,0:T(8,128)(2,1)S(1)}, bf16[768,256]{1,0:T(8,128)(2,1)S(1)}, u32[]{:S(2)}, u32[]{:S(2)}) collective-permute-start(bf16[768,256]{1,0:T(8,128)(2,1)S(1)} %get-tuple-element.76.refs_0_), channel_id=1, source_target_pairs={{0,6},{2,0},{4,2},{6,4},{1,7},{3,1},{5,3},{7,5},{8,14},{10,8},{12,... | collective-permute-start | bytes 1179656 | tf_op jit(solution)/shard_map/ppermute | solution.py:66
  2.7 19.8 %collective-permute-start.7 = (bf16[768,256]{1,0:T(8,128)(2,1)S(1)}, bf16[768,256]{1,0:T(8,128)(2,1)S(1)}, u32[]{:S(2)}, u32[]{:S(2)}) collective-permute-start(bf16[768,256]{1,0:T(8,128)(2,1)S(1)} %get-tuple-element.76.refs_0_), channel_id=1, source_target_pairs={{0,4},{2,6},{4,0},{6,2},{1,5},{3,7},{5,1},{7,3},{8,12},{10,14},{12... | collective-permute-start | bytes 1179656 | tf_op jit(solution)/shard_map/ppermute | solution.py:66
  3.6 23.2 %collective-permute-start.8 = (bf16[768,256]{1,0:T(8,128)(2,1)S(1)}, bf16[768,256]{1,0:T(8,128)(2,1)S(1)}, u32[]{:S(2)}, u32[]{:S(2)}) collective-permute-start(bf16[768,256]{1,0:T(8,128)(2,1)S(1)} %get-tuple-element.76.refs_0_), channel_id=1, source_target_pairs={{0,2},{2,4},{4,6},{6,0},{1,3},{3,5},{5,7},{7,1},{8,10},{10,12},{12... | collective-permute-start | bytes 1179656 | tf_op jit(solution)/shard_map/ppermute | solution.py:66
  7.7 15.2 %collective-permute-start.1 = (f32[48,256]{1,0:T(8,128)S(1)}, f32[48,256]{1,0:T(8,128)S(1)}, u32[]{:S(2)}, u32[]{:S(2)}) collective-permute-start(f32[48,256]{1,0:T(8,128)S(1)} %get-tuple-element.74.refs_0_), channel_id=1, source_target_pairs={{0,96},{32,0},{64,32},{96,64},{1,97},{33,1},{65,33},{97,65},{2,98}... | collective-permute-start | bytes 147464 | tf_op jit(solution)/shard_map/ppermute | solution.py:113
  11.9 47.1 %collective-permute-start.9 = (bf16[768,256]{1,0:T(8,128)(2,1)S(1)}, bf16[768,256]{1,0:T(8,128)(2,1)S(1)}, u32[]{:S(2)}, u32[]{:S(2)}) collective-permute-start(bf16[768,256]{1,0:T(8,128)(2,1)S(1)} %get-tuple-element.76.refs_0_), channel_id=1, source_target_pairs={{0,1},{1,0},{2,3},{3,2},{4,5},{5,4},{6,7},{7,6},{8,9},{9,8},{10,11... | collective-permute-start | bytes 1179656 | tf_op jit(solution)/shard_map/ppermute | solution.py:70
  22.4 37.1 %collective-permute-start.10 = (bf16[768,256]{1,0:T(8,128)(2,1)S(1)}, bf16[768,256]{1,0:T(8,128)(2,1)S(1)}, u32[]{:S(2)}, u32[]{:S(2)}) collective-permute-start(bf16[768,256]{1,0:T(8,128)(2,1)S(1)} %collective-permute-done.6.refs_1_), channel_id=1, source_target_pairs={{0,1},{1,0},{2,3},{3,2},{4,5},{5,4},{6,7},{7,6},{8,9},{9,8},{10,11... | collective-permute-start | bytes 1179656 | tf_op jit(solution)/shard_map/ppermute | solution.py:70
  22.5 37.2 %collective-permute-start.11 = (bf16[768,256]{1,0:T(8,128)(2,1)S(1)}, bf16[768,256]{1,0:T(8,128)(2,1)S(1)}, u32[]{:S(2)}, u32[]{:S(2)}) collective-permute-start(bf16[768,256]{1,0:T(8,128)(2,1)S(1)} %collective-permute-done.7.refs_2_), channel_id=1, source_target_pairs={{0,1},{1,0},{2,3},{3,2},{4,5},{5,4},{6,7},{7,6},{8,9},{9,8},{10,11... | collective-permute-start | bytes 1179656 | tf_op jit(solution)/shard_map/ppermute | solution.py:70
  26.8 39.0 %collective-permute-start.12 = (bf16[768,256]{1,0:T(8,128)(2,1)S(1)}, bf16[768,256]{1,0:T(8,128)(2,1)S(1)}, u32[]{:S(2)}, u32[]{:S(2)}) collective-permute-start(bf16[768,256]{1,0:T(8,128)(2,1)S(1)} %collective-permute-done.8.refs_3_), channel_id=1, source_target_pairs={{0,1},{1,0},{2,3},{3,2},{4,5},{5,4},{6,7},{7,6},{8,9},{9,8},{10,11... | collective-permute-start | bytes 1179656 | tf_op jit(solution)/shard_map/ppermute | solution.py:70
  72.2 27.4 %collective-permute-start.48 = (bf16[512,640]{1,0:T(8,128)(2,1)S(1)}, bf16[512,640]{1,0:T(8,128)(2,1)S(1)}, u32[]{:S(2)}, u32[]{:S(2)}) collective-permute-start(bf16[512,640]{1,0:T(8,128)(2,1)S(1)} %get-tuple-element.130), channel_id=1, source_target_pairs={{0,24},{8,16},{16,8},{24,0},{1,25},{9,17},{17,9},{25,1},{2,26},{10... | collective-permute-start | bytes 1966088 | tf_op jit(solution)/shard_map/ppermute | solution.py:606
  76.6 29.3 %collective-permute-start.42 = (bf16[512,768]{1,0:T(8,128)(2,1)S(1)}, bf16[512,768]{1,0:T(8,128)(2,1)S(1)}, u32[]{:S(2)}, u32[]{:S(2)}) collective-permute-start(bf16[512,768]{1,0:T(8,128)(2,1)S(1)} %get-tuple-element.123), channel_id=1, source_target_pairs={{0,8},{8,0},{16,24},{24,16},{1,9},{9,1},{17,25},{25,17},{2,10},{10... | collective-permute-start | bytes 2359304 | tf_op jit(solution)/shard_map/ppermute | solution.py:606
  76.7 36.1 %collective-permute-start.41 = (bf16[512,768]{1,0:T(8,128)(2,1)S(1)}, bf16[512,768]{1,0:T(8,128)(2,1)S(1)}, u32[]{:S(2)}, u32[]{:S(2)}) collective-permute-start(bf16[512,768]{1,0:T(8,128)(2,1)S(1)} %get-tuple-element.122), channel_id=1, source_target_pairs={{0,8},{8,0},{16,24},{24,16},{1,9},{9,1},{17,25},{25,17},{2,10},{10... | collective-permute-start | bytes 2359304 | tf_op jit(solution)/shard_map/ppermute | solution.py:607
  78.7 25.7 %collective-permute-start.47 = (bf16[512,640]{1,0:T(8,128)(2,1)S(1)}, bf16[512,640]{1,0:T(8,128)(2,1)S(1)}, u32[]{:S(2)}, u32[]{:S(2)}) collective-permute-start(bf16[512,640]{1,0:T(8,128)(2,1)S(1)} %get-tuple-element.129), channel_id=1, source_target_pairs={{0,24},{8,16},{16,8},{24,0},{1,25},{9,17},{17,9},{25,1},{2,26},{10... | collective-permute-start | bytes 1966088 | tf_op jit(solution)/shard_map/ppermute | solution.py:607
  81.5 17.7 %collective-permute-start.29 = (bf16[1024,128]{1,0:T(8,128)(2,1)S(1)}, bf16[1024,128]{1,0:T(8,128)(2,1)S(1)}, u32[]{:S(2)}, u32[]{:S(2)}) collective-permute-start(bf16[1024,128]{1,0:T(8,128)(2,1)S(1)} %get-tuple-element.108), channel_id=1, source_target_pairs={{0,32},{32,0},{64,96},{96,64},{1,33},{33,1},{65,97},{97,65},{2,34}... | collective-permute-start | bytes 786440 | tf_op jit(solution)/shard_map/ppermute | solution.py:605
  99.3 55.1 %collective-permute-start.20 = (bf16[8,256,384]{2,1,0:T(8,128)(2,1)S(1)}, bf16[8,256,384]{2,1,0:T(8,128)(2,1)S(1)}, u32[]{:S(2)}, u32[]{:S(2)}) collective-permute-start(bf16[8,256,384]{2,1,0:T(8,128)(2,1)S(1)} %get-tuple-element.97), channel_id=1, source_target_pairs={{0,1},{1,0},{2,3},{3,2},{4,5},{5,4},{6,7},{7,6},{8,9},{9,8},{10,11... | collective-permute-start | bytes 4718600 | tf_op jit(solution)/shard_map/ppermute | solution.py:455
  99.6 21.7 %collective-permute-start.36 = (bf16[512,768]{1,0:T(8,128)(2,1)S(1)}, bf16[512,768]{1,0:T(8,128)(2,1)S(1)}, u32[]{:S(2)}, u32[]{:S(2)}) collective-permute-start(bf16[512,768]{1,0:T(8,128)(2,1)S(1)} %get-tuple-element.116), channel_id=1, source_target_pairs={{0,96},{32,64},{64,32},{96,0},{1,97},{33,65},{65,33},{97,1},{2,98}... | collective-permute-start | bytes 2359304 | tf_op jit(solution)/shard_map/ppermute | solution.py:606
  104.4 20.4 %collective-permute-start.30 = (bf16[512,768]{1,0:T(8,128)(2,1)S(1)}, bf16[512,768]{1,0:T(8,128)(2,1)S(1)}, u32[]{:S(2)}, u32[]{:S(2)}) collective-permute-start(bf16[512,768]{1,0:T(8,128)(2,1)S(1)} %get-tuple-element.109), channel_id=1, source_target_pairs={{0,32},{32,0},{64,96},{96,64},{1,33},{33,1},{65,97},{97,65},{2,34}... | collective-permute-start | bytes 2359304 | tf_op jit(solution)/shard_map/ppermute | solution.py:606
  106.0 31.6 %collective-permute-start.35 = (bf16[512,768]{1,0:T(8,128)(2,1)S(1)}, bf16[512,768]{1,0:T(8,128)(2,1)S(1)}, u32[]{:S(2)}, u32[]{:S(2)}) collective-permute-start(bf16[512,768]{1,0:T(8,128)(2,1)S(1)} %get-tuple-element.115), channel_id=1, source_target_pairs={{0,96},{32,64},{64,32},{96,0},{1,97},{33,65},{65,33},{97,1},{2,98}... | collective-permute-start | bytes 2359304 | tf_op jit(solution)/shard_map/ppermute | solution.py:607
  112.8 27.3 %collective-permute-start.28 = (bf16[512,768]{1,0:T(8,128)(2,1)S(1)}, bf16[512,768]{1,0:T(8,128)(2,1)S(1)}, u32[]{:S(2)}, u32[]{:S(2)}) collective-permute-start(bf16[512,768]{1,0:T(8,128)(2,1)S(1)} %get-tuple-element.106), channel_id=1, source_target_pairs={{0,32},{32,0},{64,96},{96,64},{1,33},{33,1},{65,97},{97,65},{2,34}... | collective-permute-start | bytes 2359304 | tf_op jit(solution)/shard_map/ppermute | solution.py:607
  121.3 19.5 %collective-permute-start.50 = (bf16[256,640]{1,0:T(8,128)(2,1)S(1)}, bf16[256,640]{1,0:T(8,128)(2,1)S(1)}, u32[]{:S(2)}, u32[]{:S(2)}) collective-permute-start(bf16[256,640]{1,0:T(8,128)(2,1)S(1)} %get-tuple-element.132), channel_id=1, source_target_pairs={{0,8},{8,0},{16,24},{24,16},{1,9},{9,1},{17,25},{25,17},{2,10},{10... | collective-permute-start | bytes 983048 | tf_op jit(solution)/shard_map/ppermute | solution.py:609
  124.8 17.4 %collective-permute-start.44 = (bf16[256,768]{1,0:T(8,128)(2,1)S(1)}, bf16[256,768]{1,0:T(8,128)(2,1)S(1)}, u32[]{:S(2)}, u32[]{:S(2)}) collective-permute-start(bf16[256,768]{1,0:T(8,128)(2,1)S(1)} %get-tuple-element.125), channel_id=1, source_target_pairs={{0,24},{8,16},{16,8},{24,0},{1,25},{9,17},{17,9},{25,1},{2,26},{10... | collective-permute-start | bytes 1179656 | tf_op jit(solution)/shard_map/ppermute | solution.py:609
  137.6 15.0 %collective-permute-start.32 = (bf16[256,896]{1,0:T(8,128)(2,1)S(1)}, bf16[256,896]{1,0:T(8,128)(2,1)S(1)}, u32[]{:S(2)}, u32[]{:S(2)}) collective-permute-start(bf16[256,896]{1,0:T(8,128)(2,1)S(1)} %get-tuple-element.111), channel_id=1, source_target_pairs={{0,96},{32,64},{64,32},{96,0},{1,97},{33,65},{65,33},{97,1},{2,98}... | collective-permute-start | bytes 1376264 | tf_op jit(solution)/shard_map/ppermute | solution.py:609
  142.3 21.4 %collective-permute-start.31 = (bf16[256,896]{1,0:T(8,128)(2,1)S(1)}, bf16[256,896]{1,0:T(8,128)(2,1)S(1)}, u32[]{:S(2)}, u32[]{:S(2)}) collective-permute-start(bf16[256,896]{1,0:T(8,128)(2,1)S(1)} %get-tuple-element.110), channel_id=1, source_target_pairs={{0,96},{32,64},{64,32},{96,0},{1,97},{33,65},{65,33},{97,1},{2,98}... | collective-permute-start | bytes 1376264 | tf_op jit(solution)/shard_map/ppermute | solution.py:610
  152.6 16.9 %collective-permute-start.45 = (bf16[256,768]{1,0:T(8,128)(2,1)S(1)}, bf16[256,768]{1,0:T(8,128)(2,1)S(1)}, u32[]{:S(2)}, u32[]{:S(2)}) collective-permute-start(bf16[256,768]{1,0:T(8,128)(2,1)S(1)} %half_add.27), channel_id=1, source_target_pairs={{0,32},{32,0},{64,96},{96,64},{1,33},{33,1},{65,97},{97,65},{2,34}... | collective-permute-start | bytes 1179656 | tf_op jit(solution)/shard_map/ppermute | solution.py:613
  154.4 16.1 %collective-permute-start.33 = (bf16[256,896]{1,0:T(8,128)(2,1)S(1)}, bf16[256,896]{1,0:T(8,128)(2,1)S(1)}, u32[]{:S(2)}, u32[]{:S(2)}) collective-permute-start(bf16[256,896]{1,0:T(8,128)(2,1)S(1)} %half_add.19), channel_id=1, source_target_pairs={{0,8},{8,0},{16,24},{24,16},{1,9},{9,1},{17,25},{25,17},{2,10},{10... | collective-permute-start | bytes 1376264 | tf_op jit(solution)/shard_map/ppermute | solution.py:613
  154.9 15.9 %collective-permute-start.21 = (bf16[512,384]{1,0:T(8,128)(2,1)S(1)}, bf16[512,384]{1,0:T(8,128)(2,1)S(1)}, u32[]{:S(2)}, u32[]{:S(2)}) collective-permute-start(bf16[512,384]{1,0:T(8,128)(2,1)S(1)} %get-tuple-element.99), channel_id=1, source_target_pairs={{0,2},{2,4},{4,6},{6,0},{1,3},{3,5},{5,7},{7,1},{8,10},{10,12},{12... | collective-permute-start | bytes 1179656 | tf_op jit(solution)/shard_map/ppermute | solution.py:468
  163.6 15.7 %collective-permute-start.22 = (bf16[512,384]{1,0:T(8,128)(2,1)S(1)}, bf16[512,384]{1,0:T(8,128)(2,1)S(1)}, u32[]{:S(2)}, u32[]{:S(2)}) collective-permute-start(bf16[512,384]{1,0:T(8,128)(2,1)S(1)} %get-tuple-element.100), channel_id=1, source_target_pairs={{0,6},{2,0},{4,2},{6,4},{1,7},{3,1},{5,3},{7,5},{8,14},{10,8},{12,... | collective-permute-start | bytes 1179656 | tf_op jit(solution)/shard_map/ppermute | solution.py:468
  163.6 17.5 %collective-permute-start.23 = (bf16[512,384]{1,0:T(8,128)(2,1)S(1)}, bf16[512,384]{1,0:T(8,128)(2,1)S(1)}, u32[]{:S(2)}, u32[]{:S(2)}) collective-permute-start(bf16[512,384]{1,0:T(8,128)(2,1)S(1)} %get-tuple-element.101), channel_id=1, source_target_pairs={{0,4},{2,6},{4,0},{6,2},{1,5},{3,7},{5,1},{7,3},{8,12},{10,14},{12... | collective-permute-start | bytes 1179656 | tf_op jit(solution)/shard_map/ppermute | solution.py:468
  169.5 15.2 %collective-permute-start.39 = (bf16[256,768]{1,0:T(8,128)(2,1)S(1)}, bf16[256,768]{1,0:T(8,128)(2,1)S(1)}, u32[]{:S(2)}, u32[]{:S(2)}) collective-permute-start(bf16[256,768]{1,0:T(8,128)(2,1)S(1)} %half_add.23), channel_id=1, source_target_pairs={{0,24},{8,16},{16,8},{24,0},{1,25},{9,17},{17,9},{25,1},{2,26},{10... | collective-permute-start | bytes 1179656 | tf_op jit(solution)/shard_map/ppermute | solution.py:613
  179.3 20.8 %collective-permute-start.34 = (bf16[128,896]{1,0:T(8,128)(2,1)S(1)}, bf16[128,896]{1,0:T(8,128)(2,1)S(1)}, u32[]{:S(2)}, u32[]{:S(2)}) collective-permute-start(bf16[128,896]{1,0:T(8,128)(2,1)S(1)} %get-tuple-element.113), channel_id=1, source_target_pairs={{0,24},{8,16},{16,8},{24,0},{1,25},{9,17},{17,9},{25,1},{2,26},{10... | collective-permute-start | bytes 688136 | tf_op jit(solution)/shard_map/ppermute | solution.py:616
  181.1 18.9 %collective-permute-start.46 = (bf16[128,768]{1,0:T(8,128)(2,1)S(1)}, bf16[128,768]{1,0:T(8,128)(2,1)S(1)}, u32[]{:S(2)}, u32[]{:S(2)}) collective-permute-start(bf16[128,768]{1,0:T(8,128)(2,1)S(1)} %get-tuple-element.127), channel_id=1, source_target_pairs={{0,96},{32,64},{64,32},{96,0},{1,97},{33,65},{65,33},{97,1},{2,98}... | collective-permute-start | bytes 589832 | tf_op jit(solution)/shard_map/ppermute | solution.py:616
  184.9 15.2 %collective-permute-start.40 = (bf16[128,768]{1,0:T(8,128)(2,1)S(1)}, bf16[128,768]{1,0:T(8,128)(2,1)S(1)}, u32[]{:S(2)}, u32[]{:S(2)}) collective-permute-start(bf16[128,768]{1,0:T(8,128)(2,1)S(1)} %get-tuple-element.120), channel_id=1, source_target_pairs={{0,8},{8,0},{16,24},{24,16},{1,9},{9,1},{17,25},{25,17},{2,10},{10... | collective-permute-start | bytes 589832 | tf_op jit(solution)/shard_map/ppermute | solution.py:616
  185.2 14.9 %collective-permute-start.52 = (bf16[128,640]{1,0:T(8,128)(2,1)S(1)}, bf16[128,640]{1,0:T(8,128)(2,1)S(1)}, u32[]{:S(2)}, u32[]{:S(2)}) collective-permute-start(bf16[128,640]{1,0:T(8,128)(2,1)S(1)} %get-tuple-element.134), channel_id=1, source_target_pairs={{0,32},{32,0},{64,96},{96,64},{1,33},{33,1},{65,97},{97,65},{2,34}... | collective-permute-start | bytes 491528 | tf_op jit(solution)/shard_map/ppermute | solution.py:616
  (24 other events, 180.4 us)
